TPU v7x, 256 devices: a whole 4x4x8 slice. The times are simulated.
256 devices in a mesh: seq: 32 (over x, z), head: 8 (over y, core).
Axes of the slice: x: 4, y: 4, z: 8, core: 2. Of those that a mesh axis runs over, the one named last changes fastest.
Arguments:
- queries: bfloat16 [32768, 4096], P('seq', 'head'), may hold values from -150 to 150
- keys: bfloat16 [32768, 4096], P('seq', 'head'), may hold values from -7 to 7
- values: bfloat16 [32768, 4096], P('seq', 'head'), may hold values from -6 to 6
- random_holder: int32 [32, 256, 3], P('head', 'seq'), may hold values from 0 to 31, all different within a row; in each aligned block of 8 rows (0 to 7, 8 to 15, ..., all dimensions but the last counted through in order) at most 2 rows name the same one
- random_offset: int32 [32, 256, 3], P('head', 'seq'), may hold values from 0 to 7
- keep: int32 [256], P('seq'), may hold values from 0 to 1, as said below
Outputs:
- packed: bfloat16 [32768, 4096], P('seq', 'head')
Inputs may be any that keep to these rules, and one draw needn't show every extreme that they name: `random_holder`: for each head, the 8 query blocks of one index of seq name no index of seq more than 2 times over all their random entries; the 3 entries of one query block and head differ. `keep`: block j is kept where j % 8 == 0 or j % 8 == 7, and not kept where j % 8 == 1.
All inputs are finite; a program needn't handle non-finite values.
Results may differ from a plain program's by a relative error of at most 0.007.
Values may be sent and summed in bfloat16 or wider, within the bound.
A program may use at most 128 MiB of HBM per device.

v0:
```python
import functools
import math

import jax
import jax.numpy as jnp
from jax import lax
from jax.sharding import PartitionSpec as P

DH = 128
B = 128
G = 2
R = 3


neg_big = -1e30


def extended_2(block, sides, width):
    for axis, dim in sides:
        count = lax.axis_size(axis)
        forward = [(i, i + 1) for i in range(count - 1)]
        backward = [(target, source) for source, target in forward]
        low = lax.ppermute(
            lax.slice_in_dim(block, block.shape[dim] - width, None, axis=dim), axis, forward
        )
        high = lax.ppermute(lax.slice_in_dim(block, 0, width, axis=dim), axis, backward)
        block = jnp.concatenate([low, block, high], axis=dim)
    return block


def filled_up(lines, size):
    spare = -len(lines) % size
    return jnp.pad(lines, [(0, spare)] + [(0, 0)] * (lines.ndim - 1))


def spread(x, axis, root):
    lines = jnp.where(lax.axis_index(axis) == root, x, jnp.zeros_like(x)).reshape(
        -1, *x.shape[1:][-1:]
    )
    padded = filled_up(lines, lax.axis_size(axis))
    own = lax.psum_scatter(padded, axis, scatter_dimension=0, tiled=True)
    return lax.all_gather(own, axis, axis=0, tiled=True)[: len(lines)].reshape(x.shape)


def sent_to_all(x, axis):
    size = lax.axis_size(axis)
    return lax.all_to_all(jnp.broadcast_to(x[None], (size, *x.shape)), axis, 0, 0, tiled=True)


def combined_pairwise(pieces, combine):
    while len(jax.tree.leaves(pieces)[0]) > 1:
        pieces = jax.vmap(combine)(*(pieces[side::2] for side in (0, 1)))
    return pieces[0]


def prefix(x, axis, combine, identity):
    size, position = (lax.axis_size(axis), lax.axis_index(axis))
    passed = jnp.arange(size) < position

    def kept(part, zero, own):
        part = jnp.where(
            passed.reshape(-1, *(1 for _ in own.shape)), part, jnp.asarray(zero, own.dtype)
        )
        return part

    pieces = sent_to_all(x, axis)
    return combined_pairwise(kept(pieces, identity, x), combine)


def shifted(x, axis, by):
    size = lax.axis_size(axis)
    pairs = [(i, i + by) for i in range(size) if 0 <= i + by < size]
    return lax.ppermute(x, axis, pairs)


def tile_stats(query_blocks, key_tile, value_tile, spec_scores, spec_out, score_scale):
    scores = (
        jnp.einsum(spec_scores, query_blocks, key_tile, preferred_element_type=jnp.float32)
        * score_scale
    )
    row_max = jnp.max(scores, axis=-1)
    weights = jnp.exp(scores - row_max[..., None]).astype(jnp.bfloat16)
    row_sum = jnp.sum(weights, axis=-1, dtype=jnp.float32)
    summed = jnp.einsum(spec_out, weights, value_tile, preferred_element_type=jnp.float32)
    return (row_max, row_sum, summed)


def merge_tiles(parts):
    peaks = [jnp.where(live, row_max, neg_big) for live, row_max, row_sum, summed in parts]
    overall = functools.reduce(jnp.maximum, peaks)
    numer = jnp.zeros(parts[0][3].shape, jnp.float32)
    denom = jnp.zeros(parts[0][1].shape, jnp.float32)
    for live, row_max, row_sum, summed in parts:
        factor = jnp.where(live, jnp.exp(row_max - overall), 0.0)
        numer = numer + factor[..., None] * summed
        denom = denom + factor * row_sum
    return numer / denom[..., None]


def add_counts(earlier, later):
    return earlier + later


def body(queries, keys, values, random_holder, random_offset, keep):
    tok_dev, width_dev = queries.shape
    blk_dev = tok_dev // B
    head_dev = width_dev // DH
    seq_count = lax.axis_size("seq")
    my_index = lax.axis_index("seq")
    score_scale = 1.0 / math.sqrt(DH)
    query_blocks = queries.reshape(blk_dev, B, head_dev, DH)
    key_value = jnp.stack((keys, values))
    block_ids = my_index * blk_dev + jnp.arange(blk_dev, dtype=jnp.int32)
    extended = extended_2(key_value, (("seq", 1),), B)
    parts = []
    for shift_by in (-1, 0, 1):
        near_tiles = lax.slice_in_dim(
            extended, (1 + shift_by) * B, (1 + shift_by) * B + tok_dev, axis=1
        )
        near_tiles = near_tiles.reshape(2, blk_dev, B, head_dev, DH)
        neighbour = block_ids + shift_by
        live = ((neighbour >= 0) & (neighbour < blk_dev * seq_count))[:, None, None]
        parts.append(
            (live,)
            + tile_stats(
                query_blocks,
                near_tiles[0],
                near_tiles[1],
                "nqhd,nkhd->nqhk",
                "nqhk,nkhd->nqhd",
                score_scale,
            )
        )
    shared = spread(key_value[:, : G * B], "seq", 0).reshape(2, G, B, head_dev, DH)
    for glob_pos in range(G):
        parts.append(
            (True,)
            + tile_stats(
                query_blocks,
                shared[0, glob_pos],
                shared[1, glob_pos],
                "nqhd,khd->nqhk",
                "nqhk,khd->nqhd",
                score_scale,
            )
        )
    count_req = blk_dev * R
    capacity = max(2, (count_req + seq_count - 1) // seq_count)
    holders = random_holder.reshape(head_dev, count_req)
    offset_idx = random_offset.reshape(head_dev, count_req)
    onehot = (holders[..., None] == jnp.arange(seq_count, dtype=jnp.int32)).astype(jnp.int32)
    rank = jnp.sum((jnp.cumsum(onehot, axis=1) - onehot) * onehot, axis=-1)
    selector = onehot[..., None] * (
        rank[:, :, None, None] == jnp.arange(capacity, dtype=jnp.int32)
    ).astype(jnp.int32)
    asked_slots = jnp.transpose(
        jnp.sum(selector * (offset_idx + 1)[:, :, None, None], axis=1), (1, 0, 2)
    )
    tiles_kv = key_value.reshape(2, blk_dev, B, head_dev, DH)
    asked = lax.all_to_all(asked_slots, "seq", split_axis=0, concat_axis=0, tiled=True)
    entry = jnp.maximum(asked - 1, 0)
    head_idx = jnp.arange(asked.shape[1], dtype=jnp.int32)[None, :, None]
    picked = tiles_kv[:, entry, :, head_idx, :]
    picked = jnp.where((asked > 0)[..., None, None, None], picked, jnp.zeros_like(picked))
    replies = lax.all_to_all(picked, "seq", split_axis=0, concat_axis=0, tiled=True)
    head_rows = jnp.arange(head_dev, dtype=jnp.int32)[:, None]
    fetched = replies[holders, head_rows, rank].reshape(head_dev, blk_dev, R, 2, B, DH)
    for rand_pos in range(R):
        parts.append(
            (True,)
            + tile_stats(
                query_blocks,
                fetched[:, :, rand_pos, 0],
                fetched[:, :, rand_pos, 1],
                "nqhd,hnkd->nqhk",
                "nqhk,hnkd->nqhd",
                score_scale,
            )
        )
    attended = merge_tiles(parts).astype(jnp.bfloat16).reshape(blk_dev, B * width_dev)
    kept_count = jnp.sum(keep)
    start_rank = prefix(kept_count, "seq", add_counts, jnp.int32(0))
    local_rank = jnp.cumsum(keep) - keep
    target = start_rank + local_rank
    blocks = jnp.where((keep > 0)[:, None], attended, jnp.zeros_like(attended))
    slot = target % blk_dev
    distance = jnp.where(keep > 0, my_index - target // blk_dev, 0)
    placing = (slot[None, :] == jnp.arange(blk_dev, dtype=jnp.int32)[:, None]) & (keep > 0)[None, :]
    blocks = jnp.dot(
        placing.astype(jnp.bfloat16), blocks, preferred_element_type=jnp.float32
    ).astype(jnp.bfloat16)
    distance = jnp.sum(placing.astype(jnp.int32) * distance[None, :], axis=1)
    for bit_pos in range((seq_count - 1).bit_length()):
        stride = 2**bit_pos
        moving = distance // stride % 2 > 0
        moved = jnp.where(moving[:, None], blocks, jnp.zeros_like(blocks))
        moved_dist = jnp.where(moving, distance, 0).astype(jnp.bfloat16)
        staying = jnp.where(moving[:, None], jnp.zeros_like(blocks), blocks)
        staying_dist = jnp.where(moving, 0, distance)
        arrived, arrived_dist = shifted((moved, moved_dist), "seq", -stride)
        blocks = staying + arrived
        distance = staying_dist + arrived_dist.astype(jnp.int32)
    return blocks.reshape(tok_dev, width_dev)


def solution(mesh):
    in_specs = (
        P("seq", "head"),
        P("seq", "head"),
        P("seq", "head"),
        P("head", "seq", None),
        P("head", "seq", None),
        P("seq"),
    )
    out_specs = P("seq", "head")
    return jax.shard_map(body, mesh=mesh, in_specs=in_specs, out_specs=out_specs, check_vma=False)
```

profile of v0, /device:TPU:226, one launch (start us, length us, event | category | flops | bytes accessed | tf_op | source)
XLA Modules:
  0.0 766.5 jit_solution(5515449604694585865)
XLA Ops:
  9.5 8.4 %all-to-all-start.1 = ((s32[32,4,2]{1,2,0:T(2,128)}), s32[32,4,2]{1,2,0:T(2,128)S(1)}, u32[]{:S(2)}, u32[]{:S(2)}) async-start(s32[32,4,2]{1,2,0:T(2,128)} %copy.377), calls=%async_computation.2 | async-start | bytes 65536 | tf_op jit(solution)/shard_map/all_to_all | solution.py:160
  25.7 8.7 %all-to-all-start = ((s32[32,1,1]{2,1,0:T(1,128)}), s32[32,1,1]{2,1,0:T(1,128)S(1)}, u32[]{:S(2)}, u32[]{:S(2)}) async-start(s32[32,1,1]{2,1,0:T(1,128)} %broadcast_in_dim.190), calls=%async_computation | async-start | bytes 32768 | tf_op jit(solution)/shard_map/all_to_all | solution.py:47
  35.0 10.0 %gather_fusion = bf16[256,2,128,128]{3,2,1,0:T(8,128)(2,1)} fusion(bf16[2,8,128,4,128]{4,2,3,1,0:T(8,128)(2,1)S(1)} %pad_maximum_fusion, s32[256]{0:T(256)S(1)} %reshape.400), kind=kCustom, calls=%fused_computation | custom fusion | bytes 33556480 | tf_op jit(solution)/shard_map/gather | solution.py:163
  45.0 14.0 %broadcast_select_fusion = bf16[32,4,2,2,128,128]{5,4,3,2,1,0:T(8,128)(2,1)} fusion(bf16[32,4,2,2,128,128]{5,4,3,2,1,0:T(8,128)(2,1)} %bitcast.210, pred[32,4,2]{2,1,0:T(4,128)(4,1)S(1)} %copy.379), kind=kLoop, calls=%fused_computation.3 | loop fusion | flops 8388608 | bytes 33554688 | tf_op jit(solution)/shard_map/jit(_where)/select_n | solution.py:164
  59.0 10.0 %all-to-all-start.2 = ((bf16[32,4,2,2,128,128]{5,4,3,2,1,0:T(8,128)(2,1)}), bf16[32,4,2,2,128,128]{5,4,3,2,1,0:T(8,128)(2,1)}, u32[]{:S(2)}, u32[]{:S(2)}) async-start(bf16[32,4,2,2,128,128]{5,4,3,2,1,0:T(8,128)(2,1)} %broadcast_select_fusion), calls=%async_computation.3 | async-start | bytes 33554432 | tf_op jit(solution)/shard_map/all_to_all | solution.py:165
  69.7 3.4 collective-permute-start.4
  73.1 2.5 collective-permute-start.5
  80.5 2.2 bitcast_reduce_fusion.6
  84.0 2.0 fusion.45
  89.6 389.3 %collective-permute-done.4 = bf16[2,128,512]{2,1,0:T(8,128)(2,1)} collective-permute-done((bf16[2,128,512]{2,1,0:T(8,128)(2,1)}, bf16[2,128,512]{2,1,0:T(8,128)(2,1)}, u32[]{:S(2)}, u32[]{:S(2)}) %collective-permute-start.4) | collective-permute-done | bytes 262176 | tf_op jit(solution)/shard_map/ppermute | solution.py:23
  478.9 3.0 pad_maximum_fusion.5
  483.3 2.2 bitcast_reduce_fusion.7
  489.1 3.4 convert_reduce_fusion.6
  492.4 2.2 bitcast_reduce_fusion.5
  494.6 2.1 fusion.39
  496.7 47.2 %all_gather.3 = bf16[512,512]{1,0:T(8,128)(2,1)S(1)} all-gather(bf16[16,512]{1,0:T(8,128)(2,1)} %reduce-scatter.2.cloned.1.call-done), channel_id=1, replica_groups=mesh['seq'=32,'head'=8] {'seq'}, dimensions={0}, use_global_device_ids=true | all-gather | bytes 540672 | tf_op jit(solution)/shard_map/all_gather | solution.py:42
  550.1 14.1 %gather_fusion.1 = bf16[96,2,128,128]{3,2,1,0:T(8,128)(2,1)} fusion(bf16[32,4,2,2,128,128]{5,4,3,2,1,0:T(8,128)(2,1)} %all-to-all-done.2, s32[96]{0:T(128)S(1)} %reshape.406), kind=kCustom, calls=%fused_computation.1 | custom fusion | bytes 12584064 | tf_op jit(solution)/shard_map/gather | solution.py:167
  564.1 5.3 fusion.113
  569.5 2.2 bitcast_reduce_fusion
  571.7 2.2 bitcast_reduce_fusion.1
  573.9 2.2 bitcast_reduce_fusion.2
  577.4 2.4 copy.451
  594.4 3.1 collective-permute-start.6
  597.5 1.9 collective-permute-start
  599.4 33.4 %collective-permute-done = bf16[8]{0:T(256)(128)(2,1)S(1)} collective-permute-done((bf16[8]{0:T(256)(128)(2,1)S(1)}, bf16[8]{0:T(256)(128)(2,1)S(1)}, u32[]{:S(2)}, u32[]{:S(2)}) %collective-permute-start) | collective-permute-done | bytes 48 | tf_op jit(solution)/shard_map/ppermute | solution.py:73
  633.1 1.9 collective-permute-start.7
  635.0 1.9 collective-permute-start.1
  637.0 46.4 %collective-permute-done.1 = bf16[8]{0:T(256)(128)(2,1)S(1)} collective-permute-done((bf16[8]{0:T(256)(128)(2,1)S(1)}, bf16[8]{0:T(256)(128)(2,1)S(1)}, u32[]{:S(2)}, u32[]{:S(2)}) %collective-permute-start.1) | collective-permute-done | bytes 48 | tf_op jit(solution)/shard_map/ppermute | solution.py:73
  685.6 7.6 collective-permute-start.2
  693.3 23.1 %collective-permute-done.2 = bf16[8]{0:T(256)(128)(2,1)S(1)} collective-permute-done((bf16[8]{0:T(256)(128)(2,1)S(1)}, bf16[8]{0:T(256)(128)(2,1)S(1)}, u32[]{:S(2)}, u32[]{:S(2)}) %collective-permute-start.2) | collective-permute-done | bytes 48 | tf_op jit(solution)/shard_map/ppermute | solution.py:73
  720.5 19.0 %collective-permute-done.3 = bf16[8]{0:T(256)(128)(2,1)S(1)} collective-permute-done((bf16[8]{0:T(256)(128)(2,1)S(1)}, bf16[8]{0:T(256)(128)(2,1)S(1)}, u32[]{:S(2)}, u32[]{:S(2)}) %collective-permute-start.3) | collective-permute-done | bytes 48 | tf_op jit(solution)/shard_map/ppermute | solution.py:73
  741.1 16.9 %collective-permute-done.10 = bf16[8,65536]{1,0:T(8,128)(2,1)S(1)} collective-permute-done((bf16[8,65536]{1,0:T(8,128)(2,1)S(1)}, bf16[8,65536]{1,0:T(8,128)(2,1)S(1)}, u32[]{:S(2)}, u32[]{:S(2)}) %collective-permute-start.10) | collective-permute-done | bytes 1048608 | tf_op jit(solution)/shard_map/ppermute | solution.py:73
  (146 shorter events, 56.9 us)
Async XLA Ops:
  9.5 15.0 %all-to-all-start.1 = ((s32[32,4,2]{1,2,0:T(2,128)}), s32[32,4,2]{1,2,0:T(2,128)S(1)}, u32[]{:S(2)}, u32[]{:S(2)}) async-start(s32[32,4,2]{1,2,0:T(2,128)} %copy.377), calls=%async_computation.2 | async-start | bytes 65536 | tf_op jit(solution)/shard_map/all_to_all | solution.py:160
  17.9 2.7 copy-start
  25.7 33.2 %all-to-all-start = ((s32[32,1,1]{2,1,0:T(1,128)}), s32[32,1,1]{2,1,0:T(1,128)S(1)}, u32[]{:S(2)}, u32[]{:S(2)}) async-start(s32[32,1,1]{2,1,0:T(1,128)} %broadcast_in_dim.190), calls=%async_computation | async-start | bytes 32768 | tf_op jit(solution)/shard_map/all_to_all | solution.py:47
  59.0 10.0 %copy-start.1 = (bf16[1024,512]{1,0:T(8,128)(2,1)S(1)}, bf16[1024,512]{1,0:T(8,128)(2,1)}, u32[]{:S(2)}) copy-start(bf16[1024,512]{1,0:T(8,128)(2,1)} %param.7) | copy-start | bytes 3145732
  59.0 491.1 %all-to-all-start.2 = ((bf16[32,4,2,2,128,128]{5,4,3,2,1,0:T(8,128)(2,1)}), bf16[32,4,2,2,128,128]{5,4,3,2,1,0:T(8,128)(2,1)}, u32[]{:S(2)}, u32[]{:S(2)}) async-start(bf16[32,4,2,2,128,128]{5,4,3,2,1,0:T(8,128)(2,1)} %broadcast_select_fusion), calls=%async_computation.3 | async-start | bytes 33554432 | tf_op jit(solution)/shard_map/all_to_all | solution.py:165
  69.0 427.7 %reduce-scatter.2.cloned.1.call-start = ((), (), s32[]{:S(2)}) async-start(), calls=%async_computation.4 | async-start | bytes 540672 | tf_op jit(solution)/shard_map/reduce_scatter | solution.py:41
  69.7 409.2 %collective-permute-start.4 = (bf16[2,128,512]{2,1,0:T(8,128)(2,1)}, bf16[2,128,512]{2,1,0:T(8,128)(2,1)}, u32[]{:S(2)}, u32[]{:S(2)}) collective-permute-start(bf16[2,128,512]{2,1,0:T(8,128)(2,1)} %get-tuple-element.46), channel_id=1, source_target_pairs={{0,8},{8,16},{16,24},{24,32},{32,40},{40,48},{48,56},{56,64},{64,7... | collective-permute-start | bytes 786440 | tf_op jit(solution)/shard_map/ppermute | solution.py:23
  73.1 405.8 %collective-permute-start.5 = (bf16[2,128,512]{2,1,0:T(8,128)(2,1)S(1)}, bf16[2,128,512]{2,1,0:T(8,128)(2,1)}, u32[]{:S(2)}, u32[]{:S(2)}) collective-permute-start(bf16[2,128,512]{2,1,0:T(8,128)(2,1)S(1)} %get-tuple-element.45), channel_id=1, source_target_pairs={{8,0},{16,8},{24,16},{32,24},{40,32},{48,40},{56,48},{64,56},{72,6... | collective-permute-start | bytes 786440 | tf_op jit(solution)/shard_map/ppermute | solution.py:26
  80.5 3.6 copy-start.13
  483.3 2.2 copy-start.18
  485.5 2.5 copy-start.16
  489.1 3.4 copy-start.17
  492.4 2.2 copy-start.7
  577.4 3.7 copy-start.6
  581.2 1.9 copy-start.5
  584.3 1.6 copy-start.4
  584.3 1.9 copy-start.14
  584.3 4.7 copy-start.11
  586.2 1.6 copy-start.2
  586.2 2.9 copy-start.10
  586.2 2.9 copy-start.12
  587.7 1.8 copy-start.8
  587.7 2.4 copy-start.9
  594.4 38.5 %collective-permute-start.6 = (bf16[8,65536]{1,0:T(8,128)(2,1)S(1)}, bf16[8,65536]{1,0:T(8,128)(2,1)S(1)}, u32[]{:S(2)}, u32[]{:S(2)}) collective-permute-start(bf16[8,65536]{1,0:T(8,128)(2,1)S(1)} %get-tuple-element.71), channel_id=1, source_target_pairs={{8,0},{16,8},{24,16},{32,24},{40,32},{48,40},{56,48},{64,56},{72,6... | collective-permute-start | bytes 3145736 | tf_op jit(solution)/shard_map/ppermute | solution.py:73
  597.5 35.4 %collective-permute-start = (bf16[8]{0:T(256)(128)(2,1)S(1)}, bf16[8]{0:T(256)(128)(2,1)S(1)}, u32[]{:S(2)}, u32[]{:S(2)}) collective-permute-start(bf16[8]{0:T(256)(128)(2,1)S(1)} %get-tuple-element.31), channel_id=1, source_target_pairs={{8,0},{16,8},{24,16},{32,24},{40,32},{48,40},{56,48},{64,56},{72,6... | collective-permute-start | bytes 56 | tf_op jit(solution)/shard_map/ppermute | solution.py:73
  633.1 50.3 %collective-permute-start.7 = (bf16[8,65536]{1,0:T(8,128)(2,1)S(1)}, bf16[8,65536]{1,0:T(8,128)(2,1)S(1)}, u32[]{:S(2)}, u32[]{:S(2)}) collective-permute-start(bf16[8,65536]{1,0:T(8,128)(2,1)S(1)} %broadcast_select_fusion.2), channel_id=1, source_target_pairs={{16,0},{24,8},{32,16},{40,24},{48,32},{56,40},{64,48},{72,56},{80,... | collective-permute-start | bytes 3145736 | tf_op jit(solution)/shard_map/ppermute | solution.py:73
  635.0 48.4 %collective-permute-start.1 = (bf16[8]{0:T(256)(128)(2,1)S(1)}, bf16[8]{0:T(256)(128)(2,1)S(1)}, u32[]{:S(2)}, u32[]{:S(2)}) collective-permute-start(bf16[8]{0:T(256)(128)(2,1)S(1)} %get-tuple-element.28), channel_id=1, source_target_pairs={{16,0},{24,8},{32,16},{40,24},{48,32},{56,40},{64,48},{72,56},{80,... | collective-permute-start | bytes 56 | tf_op jit(solution)/shard_map/ppermute | solution.py:73
  683.7 32.7 %collective-permute-start.8 = (bf16[8,65536]{1,0:T(8,128)(2,1)S(1)}, bf16[8,65536]{1,0:T(8,128)(2,1)S(1)}, u32[]{:S(2)}, u32[]{:S(2)}) collective-permute-start(bf16[8,65536]{1,0:T(8,128)(2,1)S(1)} %get-tuple-element.10), channel_id=1, source_target_pairs={{32,0},{40,8},{48,16},{56,24},{64,32},{72,40},{80,48},{88,56},{96,... | collective-permute-start | bytes 3145736 | tf_op jit(solution)/shard_map/ppermute | solution.py:73
  685.6 30.8 %collective-permute-start.2 = (bf16[8]{0:T(256)(128)(2,1)S(1)}, bf16[8]{0:T(256)(128)(2,1)S(1)}, u32[]{:S(2)}, u32[]{:S(2)}) collective-permute-start(bf16[8]{0:T(256)(128)(2,1)S(1)} %get-tuple-element.25), channel_id=1, source_target_pairs={{32,0},{40,8},{48,16},{56,24},{64,32},{72,40},{80,48},{88,56},{96,... | collective-permute-start | bytes 56 | tf_op jit(solution)/shard_map/ppermute | solution.py:73
  716.6 22.9 %collective-permute-start.9 = (bf16[8,65536]{1,0:T(8,128)(2,1)S(1)}, bf16[8,65536]{1,0:T(8,128)(2,1)S(1)}, u32[]{:S(2)}, u32[]{:S(2)}) collective-permute-start(bf16[8,65536]{1,0:T(8,128)(2,1)S(1)} %broadcast_select_fusion.4), channel_id=1, source_target_pairs={{64,0},{72,8},{80,16},{88,24},{96,32},{104,40},{112,48},{120,56},{... | collective-permute-start | bytes 3145736 | tf_op jit(solution)/shard_map/ppermute | solution.py:73
  718.5 20.9 %collective-permute-start.3 = (bf16[8]{0:T(256)(128)(2,1)S(1)}, bf16[8]{0:T(256)(128)(2,1)S(1)}, u32[]{:S(2)}, u32[]{:S(2)}) collective-permute-start(bf16[8]{0:T(256)(128)(2,1)S(1)} %get-tuple-element.7), channel_id=1, source_target_pairs={{64,0},{72,8},{80,16},{88,24},{96,32},{104,40},{112,48},{120,56},{... | collective-permute-start | bytes 56 | tf_op jit(solution)/shard_map/ppermute | solution.py:73
  739.8 18.2 %collective-permute-start.10 = (bf16[8,65536]{1,0:T(8,128)(2,1)S(1)}, bf16[8,65536]{1,0:T(8,128)(2,1)S(1)}, u32[]{:S(2)}, u32[]{:S(2)}) collective-permute-start(bf16[8,65536]{1,0:T(8,128)(2,1)S(1)} %get-tuple-element.5), channel_id=1, source_target_pairs={{128,0},{136,8},{144,16},{152,24},{160,32},{168,40},{176,48},{184,... | collective-permute-start | bytes 3145736 | tf_op jit(solution)/shard_map/ppermute | solution.py:73
  (4 other events, 4.5 us)
Sparse Core Ops, SparseCore 0:
  76.6 401.2 reduce-scatter.1
where the time goes:
time: 774 us; the launch traced here: 766 us
  waiting for transfers between devices  529 us (68%)
  local copies, waits for them, and re-layouts  61.4 us (8%)
  starting transfers between devices  56.6 us (7%)
  blocking collectives  47.2 us (6%)
  other arithmetic  29.7 us (4%)
  matrix products  27 us (3%)
  between operations  15.2 us (2%)
    ppermute x1, waiting for transfers between devices, extended_2(): lax.ppermute(lax.slice_in_dim(block, block.shape[dim] - width, None, axis...  389 us
    ppermute x9, waiting for transfers between devices, shifted(): return lax.ppermute(x, axis, pairs)  139 us
    all_gather x1, blocking collectives, spread(): lax.all_gather(own, axis, axis=0, tiled=True)[:len(lines)].reshape(x.shape)  47.2 us
    ppermute x9, starting transfers between devices, shifted(): return lax.ppermute(x, axis, pairs)  23.6 us
  transfers between devices with their start and end apart: 15, of which 7 were waited for; matrix products, arithmetic and copies ran while one was open for 8% of the time, Pallas kernels for 0%

commit v1 on v0

v1 whole, which is shorter than its diff:
```python
import functools
import math

import jax
import jax.numpy as jnp
from jax import lax
from jax.experimental import pallas as pl
from jax.experimental.pallas import tpu as pltpu
from jax.sharding import PartitionSpec as P

DH = 128
B = 128
G = 2
R = 3
NX = 4
NZ = 8
HD = 4
BD = 8
LCAP = 400

neg_big = -1e30
MESH = pl.DeviceIdType.MESH
SMEM_SPEC = pl.BlockSpec(memory_space=pltpu.SMEM)
VMEM_SPEC = pl.BlockSpec(memory_space=pltpu.VMEM)
score_scale = 1.0 / math.sqrt(DH)


def place():
    s = lax.axis_index("seq")
    return s, s // NZ, lax.rem(s, NZ), lax.axis_index("head")


def to_seq(s, h):
    return (s, h)


def params(cid=None, mib=48):
    if cid is None:
        return pltpu.CompilerParams(vmem_limit_bytes=mib << 20)
    return pltpu.CompilerParams(
        collective_id=cid, has_side_effects=True, vmem_limit_bytes=mib << 20
    )


def table_kernel(row, tab, send_sem, recv_sem):
    s, _, _, h = place()
    n = NX * NZ
    barrier = pltpu.get_barrier_semaphore()
    for d in range(1, n):
        pl.semaphore_signal(
            barrier, inc=1, device_id=(lax.rem(s + d, n), h), device_id_type=MESH
        )
    tab[s] = row[...]
    pl.semaphore_wait(barrier, n - 1)
    copies = []
    for d in range(1, n):
        copy = pltpu.make_async_remote_copy(
            src_ref=row,
            dst_ref=tab.at[s],
            send_sem=send_sem.at[d],
            recv_sem=recv_sem.at[d],
            device_id=(lax.rem(s + d, n), h),
            device_id_type=MESH,
        )
        copy.start()
        copies.append(copy)
    for copy in copies:
        copy.wait()


def gathered_table(row):
    n = NX * NZ
    return pl.pallas_call(
        table_kernel,
        out_shape=jax.ShapeDtypeStruct((n, 1, 128), jnp.int32),
        in_specs=[VMEM_SPEC],
        out_specs=VMEM_SPEC,
        scratch_shapes=[pltpu.SemaphoreType.DMA((n,)), pltpu.SemaphoreType.DMA((n,))],
        compiler_params=params(0, 16),
        name="table",
    )(row)


def plan_kernel(tab, send_idx, items, counts, blk, slot):
    s, x, z, _ = place()
    blk_dev = BD
    n_blocks = NX * NZ * BD

    def one(i, carry):
        rank, used, start = carry
        home = i // blk_dev
        k = tab[home, 0, HD * blk_dev * R + lax.rem(i, blk_dev)]
        used = jnp.where(lax.rem(i, blk_dev) == 0, 0, used)
        start = jnp.where(i == s * blk_dev, rank, start)
        mine = (k > 0) & (lax.rem(rank, NX) == x)
        at = jnp.where(mine, rank // NX, 64)
        blk[at] = i
        slot[at] = lax.rem(home, NZ) * 8 + (home // NZ) * 2 + used
        return rank + k, used + jnp.where(mine, 1, 0), start

    total, _, start = lax.fori_loop(0, n_blocks, one, (0, 0, 0))

    for c in range(8):
        send_idx[c] = 0
    filled = [jnp.int32(0)] * NX
    rank = start
    for j in range(blk_dev):
        k = tab[s, 0, HD * blk_dev * R + j]
        col = lax.rem(rank, NX)
        at = jnp.int32(8)
        for c in range(NX):
            hit = (k > 0) & (col == c)
            at = jnp.where(hit, c * 2 + filled[c], at)
            filled[c] = filled[c] + jnp.where(hit, 1, 0)
        send_idx[at] = j
        rank = rank + k

    def query(a, cnt):
        i = blk[a]
        home = i // blk_dev
        base = lax.rem(i, blk_dev) * R
        pos = (lax.rem(a // 2, NZ)) * 8 + (a // 16) * 2 + lax.rem(a, 2)
        word = slot[a] * 64 + pos
        cnt = list(cnt)

        def add(h, t, ok):
            w = ((t // 64) * 8 + lax.rem(t, blk_dev)) * 4096 + word
            items[h * LCAP + cnt[h]] = w
            cnt[h] = cnt[h] + jnp.where(ok, 1, 0)

        for dt in (-1, 0, 1):
            t = i + dt
            ok = (t >= 0) & (t < n_blocks) & (lax.rem(t // blk_dev, NZ) == z)
            t = jnp.clip(t, 0, n_blocks - 1)
            for h in range(HD):
                add(h, t, ok)
        for g in range(G):
            for h in range(HD):
                add(h, jnp.int32(g), z == 0)
        for h in range(HD):
            for r in range(R):
                t = tab[home, 0, h * blk_dev * R + base + r]
                add(h, t, lax.rem(t // blk_dev, NZ) == z)
        return tuple(cnt)

    n_mine = (total - x + NX - 1) // NX
    cnt = lax.fori_loop(0, n_mine, query, (jnp.int32(0),) * HD)
    for h in range(HD):
        counts[h] = cnt[h]
        for u in range(4):
            items[h * LCAP + cnt[h] + u] = jnp.int32(64)


def planned(tab):
    return pl.pallas_call(
        plan_kernel,
        out_shape=[
            jax.ShapeDtypeStruct((16,), jnp.int32),
            jax.ShapeDtypeStruct((HD * LCAP,), jnp.int32),
            jax.ShapeDtypeStruct((8,), jnp.int32),
        ],
        in_specs=[SMEM_SPEC],
        out_specs=[SMEM_SPEC] * 3,
        scratch_shapes=[pltpu.SMEM((72,), jnp.int32), pltpu.SMEM((72,), jnp.int32)],
        compiler_params=params(None, 16),
        name="plan",
    )(tab)


RING = [(k, h) for k in (1, 2, 3) for h in range(HD)]
RING_UP = RING + [(4, 0), (4, 1)]
RING_DOWN = RING + [(4, 2), (4, 3)]


def spread_kernel(idx, q, k, v, kv, qz, qs, sx, rx, so, ro, sf, rf, su, ru, sd, rd):
    s, x, z, hd = place()

    def at_x(d):
        return (lax.rem(x + d, NX) * NZ + z, hd)

    def at_z(d):
        return (x * NZ + lax.rem(z + d + NZ, NZ), hd)

    def xi(d):
        return lax.rem(x + d + NX, NX)

    def zi(d):
        return lax.rem(z + d + NZ, NZ)

    barrier = pltpu.get_barrier_semaphore()
    for d in (1, 2, 3):
        pl.semaphore_signal(barrier, inc=1, device_id=at_x(d), device_id_type=MESH)
    for d in (1, -1):
        pl.semaphore_signal(barrier, inc=1, device_id=at_z(d), device_id_type=MESH)

    def fill(c, carry):
        col, u = c // 2, lax.rem(c, 2)
        j = idx[c]
        for h in range(HD):
            qs[col, h, u] = q[j, :, h * DH : (h + 1) * DH]
        return carry

    lax.fori_loop(0, 8, fill, 0)
    for h in range(HD):
        for u in range(2):
            qz[h, z, x, u] = qs[x, h, u]
    pl.semaphore_wait(barrier, 5)

    q_out = []
    for d in (1, 2, 3):
        copy = pltpu.make_async_remote_copy(
            src_ref=qs.at[xi(d)],
            dst_ref=qz.at[:, z, x],
            send_sem=sx.at[d],
            recv_sem=rx.at[d],
            device_id=at_x(d),
            device_id_type=MESH,
        )
        copy.start()
        q_out.append(copy)

    own = []
    for h in range(HD):

        def prep(b, carry):
            rows = pl.ds(pl.multiple_of(b * B, B), B)
            kv[h, x, 0, b] = k[rows, h * DH : (h + 1) * DH]
            kv[h, x, 1, b] = v[rows, h * DH : (h + 1) * DH].T
            return carry

        lax.fori_loop(0, BD, prep, 0)
        for side, d in ((0, 1), (1, 3)):
            copy = pltpu.make_async_remote_copy(
                src_ref=kv.at[h, x],
                dst_ref=kv.at[h, x],
                send_sem=so.at[side, h],
                recv_sem=ro.at[side, h],
                device_id=at_x(d),
                device_id_type=MESH,
            )
            copy.start()
            own.append(copy)

    for d in (1, 2, 3):
        src = xi(-d)
        pltpu.make_async_remote_copy(
            src_ref=qz.at[:, z, src],
            dst_ref=qz.at[:, z, src],
            send_sem=sx.at[d],
            recv_sem=rx.at[d],
            device_id=at_x(d),
            device_id_type=MESH,
        ).wait_recv()

    rings = []

    def ring_piece(up, n):
        kk, h = (RING_UP if up else RING_DOWN)[n]
        step = -1 if up else 1
        row = zi(step * (kk - 1))
        return pltpu.make_async_remote_copy(
            src_ref=qz.at[h, row],
            dst_ref=qz.at[h, row],
            send_sem=(su if up else sd).at[n],
            recv_sem=(ru if up else rd).at[n],
            device_id=at_z(1 if up else -1),
            device_id_type=MESH,
        )

    def ring_arrival(up, n):
        kk, h = (RING_UP if up else RING_DOWN)[n]
        row = zi((-1 if up else 1) * kk)
        return pltpu.make_async_remote_copy(
            src_ref=qz.at[h, row],
            dst_ref=qz.at[h, row],
            send_sem=(su if up else sd).at[n],
            recv_sem=(ru if up else rd).at[n],
            device_id=at_z(1 if up else -1),
            device_id_type=MESH,
        )

    for n in range(4):
        for up in (True, False):
            copy = ring_piece(up, n)
            copy.start()
            rings.append(copy)

    fwd = []

    def forward_x(h):
        for side, d, part in ((0, 1, 0), (1, 3, 1)):
            src = xi(-d)
            pltpu.make_async_remote_copy(
                src_ref=kv.at[h, src],
                dst_ref=kv.at[h, src],
                send_sem=so.at[side, h],
                recv_sem=ro.at[side, h],
                device_id=at_x(d),
                device_id_type=MESH,
            ).wait_recv()
            copy = pltpu.make_async_remote_copy(
                src_ref=kv.at[h, src, part],
                dst_ref=kv.at[h, src, part],
                send_sem=sf.at[side, h],
                recv_sem=rf.at[side, h],
                device_id=at_x(d),
                device_id_type=MESH,
            )
            copy.start()
            fwd.append(copy)

    for n in range(14):
        for up in (True, False):
            kk, h = (RING_UP if up else RING_DOWN)[n]
            ring_arrival(up, n).wait_recv()
            table = RING_UP if up else RING_DOWN
            if (kk + 1, h) in table:
                copy = ring_piece(up, table.index((kk + 1, h)))
                copy.start()
                rings.append(copy)
        if n % 2 == 1 and n // 2 < HD:
            forward_x(n // 2)

    far = xi(2)
    for h in range(HD):
        for side, d, part in ((0, 1, 0), (1, 3, 1)):
            pltpu.make_async_remote_copy(
                src_ref=kv.at[h, far, part],
                dst_ref=kv.at[h, far, part],
                send_sem=sf.at[side, h],
                recv_sem=rf.at[side, h],
                device_id=at_x(d),
                device_id_type=MESH,
            ).wait_recv()
    for copy in q_out + own + rings + fwd:
        copy.wait_send()


def spread_all(idx, q, k, v):
    dma = pltpu.SemaphoreType.DMA
    return pl.pallas_call(
        spread_kernel,
        out_shape=[
            jax.ShapeDtypeStruct((HD, NX, 2, BD, B, DH), jnp.bfloat16),
            jax.ShapeDtypeStruct((HD, NZ, NX, 2, B, DH), jnp.bfloat16),
        ],
        in_specs=[SMEM_SPEC] + [VMEM_SPEC] * 3,
        out_specs=[VMEM_SPEC] * 2,
        scratch_shapes=[
            pltpu.VMEM((NX, HD, 2, B, DH), jnp.bfloat16),
            dma((4,)),
            dma((4,)),
            dma((2, HD)),
            dma((2, HD)),
            dma((2, HD)),
            dma((2, HD)),
            dma((14,)),
            dma((14,)),
            dma((14,)),
            dma((14,)),
        ],
        compiler_params=params(1),
        name="spread",
    )(idx, q, k, v)


UNROLL = 4


def part_kernel(ns, items, counts, kv, qz, out, lse, acc, top, den):
    h = pl.program_id(0)
    n_acc = NZ * ns

    def clear(a, carry):
        acc[a] = jnp.zeros((DH, B), jnp.float32)
        top[a] = jnp.full((1, B), neg_big, jnp.float32)
        den[a] = jnp.zeros((1, B), jnp.float32)
        return carry

    lax.fori_loop(0, n_acc + 1, clear, 0)

    def batch(n, carry):
        found = []
        for u in range(UNROLL):
            w = items[h * LCAP + n * UNROLL + u]
            pos = lax.rem(w, 64)
            a = (pos // 8) * ns + lax.rem(pos, 8)
            a = jnp.where(n * UNROLL + u < counts[h], a, n_acc)
            spot = lax.rem(w // 64, 64)
            tile = w // 4096
            keys = kv[0, tile // 8, 0, lax.rem(tile, 8)]
            vals = kv[0, tile // 8, 1, lax.rem(tile, 8)]
            qt = qz[0, spot // 8, lax.rem(spot, 8) // 2, lax.rem(spot, 2)]
            scores = lax.dot_general(
                keys, qt, (((1,), (1,)), ((), ())), preferred_element_type=jnp.float32
            )
            scores = scores * score_scale
            m = jnp.max(scores, axis=0, keepdims=True)
            p = jnp.exp(scores - m).astype(jnp.bfloat16)
            l = jnp.sum(p.astype(jnp.float32), axis=0, keepdims=True)
            o = jnp.dot(vals, p, preferred_element_type=jnp.float32)
            found.append((a, m, l, o))
        for a, m, l, o in found:
            old = top[a]
            new = jnp.maximum(old, m)
            f0, f1 = jnp.exp(old - new), jnp.exp(m - new)
            acc[a] = acc[a] * f0 + o * f1
            den[a] = den[a] * f0 + l * f1
            top[a] = new
        return carry

    lax.fori_loop(0, (counts[h] + UNROLL - 1) // UNROLL, batch, 0)

    def finish(a, carry):
        l = den[a]
        some = l > 0
        safe = jnp.where(some, l, 1.0)
        out[0, a // ns, lax.rem(a, ns)] = (acc[a] / safe).astype(jnp.bfloat16)
        lse[0, a // ns, lax.rem(a, ns)] = jnp.where(some, top[a] + jnp.log(safe), neg_big)
        return carry

    lax.fori_loop(0, n_acc, finish, 0)


def parts_of(ns, items, counts, kv, qz):
    n_acc = NZ * ns
    return pl.pallas_call(
        functools.partial(part_kernel, ns),
        grid=(HD,),
        out_shape=[
            jax.ShapeDtypeStruct((HD, NZ, ns, DH, B), jnp.bfloat16),
            jax.ShapeDtypeStruct((HD, NZ, ns, 1, B), jnp.float32),
        ],
        in_specs=[
            SMEM_SPEC,
            SMEM_SPEC,
            pl.BlockSpec((1, NX, 2, BD, B, DH), lambda h: (h, 0, 0, 0, 0, 0)),
            pl.BlockSpec((1, NZ, NX, 2, B, DH), lambda h: (h, 0, 0, 0, 0, 0)),
        ],
        out_specs=[
            pl.BlockSpec((1, NZ, ns, DH, B), lambda h: (h, 0, 0, 0, 0)),
            pl.BlockSpec((1, NZ, ns, 1, B), lambda h: (h, 0, 0, 0, 0)),
        ],
        scratch_shapes=[
            pltpu.VMEM((n_acc + 1, DH, B), jnp.float32),
            pltpu.VMEM((n_acc + 1, 1, B), jnp.float32),
            pltpu.VMEM((n_acc + 1, 1, B), jnp.float32),
        ],
        compiler_params=params(None, 40),
        name="parts",
    )(items, counts, kv, qz)


HOME_UP = [(4, 2), (4, 3)] + [(k, h) for k in (3, 2, 1) for h in range(HD)]
HOME_DOWN = [(4, 0), (4, 1)] + [(k, h) for k in (3, 2, 1) for h in range(HD)]


def merged(o0, l0, o1, l1):
    top = jnp.maximum(l0, l1)
    f0, f1 = jnp.exp(l0 - top), jnp.exp(l1 - top)
    both = f0 + f1
    o = (o0.astype(jnp.float32) * f0 + o1.astype(jnp.float32) * f1) / both
    return o, top + jnp.log(both)


def join_kernel(
    ns, o, lse, out, sou, slu, rou, rlu, sod, sld, rod, rld, fin, ssu, rsu, ssd, rsd, sx, rx
):
    s, x, z, hd = place()

    def at_x(d):
        return (lax.rem(x + d, NX) * NZ + z, hd)

    def at_z(d):
        return (x * NZ + lax.rem(z + d + NZ, NZ), hd)

    def zi(d):
        return lax.rem(z + d + NZ, NZ)

    barrier = pltpu.get_barrier_semaphore()
    for d in (1, 2, 3):
        pl.semaphore_signal(barrier, inc=1, device_id=at_x(d), device_id_type=MESH)
    for d in (1, -1):
        pl.semaphore_signal(barrier, inc=1, device_id=at_z(d), device_id_type=MESH)
    pl.semaphore_wait(barrier, 5)

    sent = []

    def copies(up, n, src_o, src_l):
        ro, rl = (rou, rlu) if up else (rod, rld)
        ss, rs = (ssu, rsu) if up else (ssd, rsd)
        return [
            pltpu.make_async_remote_copy(
                src_ref=src,
                dst_ref=dst.at[n],
                send_sem=ss.at[i, n],
                recv_sem=rs.at[i, n],
                device_id=at_z(1 if up else -1),
                device_id_type=MESH,
            )
            for i, (src, dst) in enumerate(((src_o, ro), (src_l, rl)))
        ]

    def send(up, n, src_o, src_l):
        for copy in copies(up, n, src_o, src_l):
            copy.start()
            sent.append(copy)

    def arrived(up, n):
        ro, rl = (rou, rlu) if up else (rod, rld)
        for copy in copies(up, n, ro.at[n], rl.at[n]):
            copy.wait_recv()

    for n in range(14):
        for up in (True, False):
            table = HOME_UP if up else HOME_DOWN
            kk, h = table[n]
            dest = zi(kk if up else -kk)
            if (kk + 1, h) not in table:
                send(up, n, o.at[h, dest], lse.at[h, dest])
                continue
            prev = table.index((kk + 1, h))
            arrived(up, prev)
            ro, rl = (rou, rlu) if up else (rod, rld)
            so, sl = (sou, slu) if up else (sod, sld)

            def step(i, carry, ro=ro, rl=rl, so=so, sl=sl, prev=prev, n=n, h=h, dest=dest):
                val, l = merged(o[h, dest, i], lse[h, dest, i], ro[prev, i], rl[prev, i])
                so[n, i] = val.astype(jnp.bfloat16)
                sl[n, i] = l
                return carry

            lax.fori_loop(0, ns, step, 0)
            send(up, n, so.at[n], sl.at[n])

    for h in range(HD):
        n = 10 + h
        arrived(True, n)
        arrived(False, n)

        def last(i, carry, h=h, n=n):
            a, la = merged(rou[n, i], rlu[n, i], rod[n, i], rld[n, i])
            val, _ = merged(o[h, z, i], lse[h, z, i], a, la)
            fin[i // 2, lax.rem(i, 2), :, h * DH : (h + 1) * DH] = val.T.astype(jnp.bfloat16)
            return carry

        lax.fori_loop(0, ns, last, 0)

    rows = ns // 2
    for r in range(NX):
        if r >= rows:

            @pl.when(x == r)
            def _():
                out[...] = jnp.zeros(out.shape, out.dtype)

            continue

        @pl.when(x == r)
        def _(r=r):
            out[:, x] = fin[r]

    def final(r, d):
        return pltpu.make_async_remote_copy(
            src_ref=fin.at[r],
            dst_ref=out.at[:, x],
            send_sem=sx.at[r],
            recv_sem=rx.at[d],
            device_id=(r * NZ + z, hd),
            device_id_type=MESH,
        )

    for d in (1, 2, 3):
        for r in range(rows):

            @pl.when(lax.rem(x + d, NX) == r)
            def _(r=r, d=d):
                final(r, d).start()

    for r in range(rows):

        @pl.when(x == r)
        def _(r=r):
            for d in (1, 2, 3):
                src = lax.rem(x - d + NX, NX)
                pltpu.make_async_remote_copy(
                    src_ref=fin.at[r],
                    dst_ref=out.at[:, src],
                    send_sem=sx.at[r],
                    recv_sem=rx.at[d],
                    device_id=at_x(d),
                    device_id_type=MESH,
                ).wait_recv()

    for d in (1, 2, 3):
        for r in range(rows):

            @pl.when(lax.rem(x + d, NX) == r)
            def _(r=r, d=d):
                final(r, d).wait_send()

    for copy in sent:
        copy.wait_send()


def joined(ns, o, lse):
    dma = pltpu.SemaphoreType.DMA
    piece_o = pltpu.VMEM((14, ns, DH, B), jnp.bfloat16)
    piece_l = pltpu.VMEM((14, ns, 1, B), jnp.float32)
    out = pl.pallas_call(
        functools.partial(join_kernel, ns),
        out_shape=jax.ShapeDtypeStruct((2, NX, B, HD * DH), jnp.bfloat16),
        in_specs=[VMEM_SPEC] * 2,
        out_specs=VMEM_SPEC,
        scratch_shapes=[
            piece_o, piece_l, piece_o, piece_l, piece_o, piece_l, piece_o, piece_l,
            pltpu.VMEM((ns // 2, 2, B, HD * DH), jnp.bfloat16),
            dma((2, 14)), dma((2, 14)), dma((2, 14)), dma((2, 14)),
            dma((4,)), dma((4,)),
        ],
        compiler_params=params(2 + ns // 8, 56),
        name="join%d" % ns,
    )(o, lse)
    return out.reshape(BD * B, HD * DH)


def body(queries, keys, values, random_holder, random_offset, keep):
    want = random_holder * BD + random_offset
    row = jnp.concatenate([want.reshape(-1), keep, jnp.zeros((24,), jnp.int32)])
    tab = gathered_table(row.reshape(1, 128))
    total = jnp.sum(tab[:, 0, HD * BD * R : HD * BD * R + BD])
    send_idx, items, counts = planned(tab)
    kv, qz = spread_all(send_idx, queries.reshape(BD, B, HD * DH), keys, values)

    def tail(ns):
        def run(items, counts, kv, qz):
            return joined(ns, *parts_of(ns, items, counts, kv, qz))

        return run

    return lax.cond(total <= 128, tail(4), tail(8), items, counts, kv, qz)


def solution(mesh):
    in_specs = (
        P("seq", "head"),
        P("seq", "head"),
        P("seq", "head"),
        P("head", "seq", None),
        P("head", "seq", None),
        P("seq"),
    )
    out_specs = P("seq", "head")
    return jax.shard_map(body, mesh=mesh, in_specs=in_specs, out_specs=out_specs, check_vma=False)
```

time: 774 us -> 280 us (0.36)
  the two profiles are of different devices: /device:TPU:226 before, /device:TPU:24 now
where the time goes in v1:
time: 280 us
  Pallas kernels  270 us (96%)
  local copies, waits for them, and re-layouts  7.44 us (3%)
    pallas_call x1, Pallas kernels, spread_all(): pl.pallas_call(spread_kernel, out_shape=[jax.ShapeDtypeStruct((HD, NX, 2,...  98.8 us
    pallas_call x1, Pallas kernels, parts_of(): pl.pallas_call(functools.partial(part_kernel, ns), grid=(HD,), out_shape=...  87.8 us
    pallas_call x1, Pallas kernels, joined(): pl.pallas_call(functools.partial(join_kernel, ns), out_shape=jax.ShapeDty...  53.1 us
    pallas_call x1, Pallas kernels, planned(): pl.pallas_call(plan_kernel, out_shape=[jax.ShapeDtypeStruct((16,), jnp.in...  15.4 us
    pallas_call x1, Pallas kernels, gathered_table(): pl.pallas_call(table_kernel, out_shape=jax.ShapeDtypeStruct((n, 1, 128),...  14.7 us

profile of v1, /device:TPU:24, one launch (start us, length us, event | category | flops | bytes accessed | tf_op | source)
XLA Modules:
  0.0 280.2 jit_solution(6549290028105806267)
XLA Ops:
  0.0 0.7 multiply_add_fusion
  0.7 0.1 copy.10
  0.8 0.1 reshape.15
  0.9 0.7 add_bitcast_fusion.row
  1.7 14.7 %table.1.tab = s32[32,1,128]{2,1,0:T(1,128)S(1)} custom-call(s32[1,128]{1,0:T(1,128)S(1)} %add_bitcast_fusion.row), custom_call_target="tpu_custom_call" | custom-call | tf_op jit(solution)/shard_map/table/pallas_call | solution.py:73
  16.4 0.7 slice_reduce_fusion
  17.8 15.4 %plan.1 = (s32[16]{0:T(128)S(1)}, s32[1600]{0:T(1024)S(1)}, s32[8]{0:T(128)S(1)}) custom-call(s32[32,1,128]{2,1,0:T(1,128)S(1)} %table.1.tab), custom_call_target="tpu_custom_call" | custom-call | tf_op jit(solution)/shard_map/plan/pallas_call | solution.py:155
  33.2 0.0 copy-start.2
  33.2 1.2 copy-done.2
  34.4 0.0 copy-start.3
  34.4 1.2 copy-done.3
  35.6 0.0 copy-start.4
  35.6 1.2 copy-done.4
  36.9 98.8 %spread.1 = (bf16[4,4,2,8,128,128]{5,4,3,2,1,0:T(8,128)(2,1)S(1)}, bf16[4,8,4,2,128,128]{5,4,3,2,1,0:T(8,128)(2,1)}) custom-call(s32[16]{0:T(128)S(1)} %get-tuple-element.43.idx, bf16[8,128,512]{2,1,0:T(8,128)(2,1)S(1)} %bitcast.5, bf16[1024,512]{1,0:T(8,128)(2,1)S(1)} %copy-done.3, bf16[1024,512]{1,0:T(8,128)(2,1)S(1)} %copy-done.4), custom_call_target="tpu_custom_call" | custom-call | tf_op jit(solution)/shard_map/spread/pallas_call | solution.py:341
  135.7 143.6 %conditional.1 = (bf16[1024,512]{1,0:T(8,128)(2,1)S(1)}) conditional(s32[]{:T(128)} %convert_element_type.3, (s32[1600]{0:T(1024)S(1)}, s32[8]{0:T(128)S(1)}, bf16[4,4,2,8,128,128]{5,4,3,2,1,0:T(8,128)(2,1)S(1)}, bf16[4,8,4,2,128,128]{5,4,3,2,1,0:T(8,128)(2,1)}) %tuple.11, (s32[1600]{0:T(1024)S(1)}, s32[8]{0:T(128)S(1)}, ...), branch_computations={%region_1.0_spmd, %region_2.0_spmd} | conditional | bytes 34078784 | solution.py:641
  135.7 87.8 %parts.3 = (bf16[4,8,4,128,128]{4,3,2,1,0:T(8,128)(2,1)S(1)}, f32[4,8,4,1,128]{4,3,2,1,0:T(1,128)S(1)}) custom-call(s32[1600]{0:T(1024)S(1)} %get-tuple-element.30.items, s32[8]{0:T(128)S(1)} %get-tuple-element.31.counts, bf16[4,4,2,8,128,128]{5,4,3,2,1,0:T(8,128)(2,1)S(1)} %get-tuple-element.32.kv, bf16[4,8,4,2,128,128]{5,4,3,2,1,0:T(8,128)(2,1)} %get-tuple-element.33.qz), custom_call_target="tpu_custom_call" | custom-call | tf_op jit(solution)/shard_map/cond/branch_1_fun/parts/pallas_call | solution.py:427
  223.5 0.0 copy-start.1
  223.5 2.0 copy-done.1
  225.5 0.0 copy-start.6
  225.5 0.6 copy-done.6
  226.1 53.1 %join4.1 = bf16[2,4,128,512]{3,2,1,0:T(8,128)(2,1)S(1)} custom-call(bf16[4,8,4,128,128]{4,3,2,1,0:T(8,128)(2,1)} %copy-done.1, f32[4,8,4,1,128]{4,3,2,1,0:T(1,128)} %copy-done.6), custom_call_target="tpu_custom_call" | custom-call | tf_op jit(solution)/shard_map/cond/branch_1_fun/join4/pallas_call | solution.py:610
  279.2 1.0 copy.14
  (1 shorter events, 0.0 us)
Async XLA Ops:
  33.2 1.2 copy-start.2
  34.4 1.2 copy-start.3
  35.6 1.2 copy-start.4
  223.5 2.0 copy-start.1
  225.5 0.6 copy-start.6

commit v2 on v1

--- a/solution.py
+++ b/solution.py
@@ -42,15 +42,31 @@
     )
 
 
-def table_kernel(row, tab, send_sem, recv_sem):
-    s, _, _, h = place()
+def first_kernel(row, k, v, tab, kv, ks, vs, send_sem, recv_sem, load, sk, rk, sf, rf):
+    s, x, z, hd = place()
     n = NX * NZ
+    loads = [
+        pltpu.make_async_copy(k.at[:, :DH], ks, load.at[0]),
+        pltpu.make_async_copy(v.at[:, :DH], vs, load.at[1]),
+    ]
+    for copy in loads:
+        copy.start()
     barrier = pltpu.get_barrier_semaphore()
     for d in range(1, n):
         pl.semaphore_signal(
-            barrier, inc=1, device_id=(lax.rem(s + d, n), h), device_id_type=MESH
+            barrier, inc=1, device_id=(lax.rem(s + d, n), hd), device_id_type=MESH
         )
     tab[s] = row[...]
+    for copy in loads:
+        copy.wait()
+
+    def prep(b, carry):
+        rows = pl.ds(pl.multiple_of(b * B, B), B)
+        kv[x, 0, b] = ks[rows, :]
+        kv[x, 1, b] = vs[rows, :].T
+        return carry
+
+    lax.fori_loop(0, BD, prep, 0)
     pl.semaphore_wait(barrier, n - 1)
     copies = []
     for d in range(1, n):
@@ -59,26 +75,645 @@
             dst_ref=tab.at[s],
             send_sem=send_sem.at[d],
             recv_sem=recv_sem.at[d],
-            device_id=(lax.rem(s + d, n), h),
+            device_id=(lax.rem(s + d, n), hd),
             device_id_type=MESH,
         )
         copy.start()
         copies.append(copy)
+
+    gather = RowGather(kv, (sk, rk, sf, rf), x, z, hd)
+    gather.own()
+    gather.forward()
+    gather.finish()
     for copy in copies:
         copy.wait()
-
-
-def gathered_table(row):
+    gather.close()
+
+
+class RowGather:
+    def __init__(self, kv, sems, x, z, hd):
+        self.kv, self.sems, self.x, self.z, self.hd = kv, sems, x, z, hd
+        self.sent = []
+
+    def piece(self, which, side, part, holder):
+        sk, rk, sf, rf = self.sems
+        ss, rs = (sk, rk) if which == 0 else (sf, rf)
+        d = 1 if side == 0 else 3
+        return pltpu.make_async_remote_copy(
+            src_ref=self.kv.at[holder, part],
+            dst_ref=self.kv.at[holder, part],
+            send_sem=ss.at[side, part],
+            recv_sem=rs.at[side, part],
+            device_id=(lax.rem(self.x + d, NX) * NZ + self.z, self.hd),
+            device_id_type=MESH,
+        )
+
+    def start(self, copy):
+        copy.start()
+        self.sent.append(copy)
+
+    def own(self):
+        for order in (0, 1):
+            for side in (0, 1):
+                self.start(self.piece(0, side, order ^ side, self.x))
+
+    def neighbour(self, side):
+        return lax.rem(self.x + (3 if side == 0 else 1), NX)
+
+    def forward(self):
+        for side in (0, 1):
+            self.piece(0, side, side, self.neighbour(side)).wait_recv()
+            self.start(self.piece(1, side, side, self.neighbour(side)))
+
+    def finish(self):
+        for side in (0, 1):
+            self.piece(0, side, 1 - side, self.neighbour(side)).wait_recv()
+        for side in (0, 1):
+            self.piece(1, side, side, lax.rem(self.x + 2, NX)).wait_recv()
+
+    def close(self):
+        for copy in self.sent:
+            copy.wait_send()
+
+
+def first_step(row, k, v):
     n = NX * NZ
+    dma = pltpu.SemaphoreType.DMA
+    any_spec = pl.BlockSpec(memory_space=pl.ANY)
     return pl.pallas_call(
-        table_kernel,
-        out_shape=jax.ShapeDtypeStruct((n, 1, 128), jnp.int32),
-        in_specs=[VMEM_SPEC],
+        first_kernel,
+        out_shape=[
+            jax.ShapeDtypeStruct((n, 1, 128), jnp.int32),
+            jax.ShapeDtypeStruct((NX, 2, BD, B, DH), jnp.bfloat16),
+        ],
+        in_specs=[VMEM_SPEC, any_spec, any_spec],
+        out_specs=[VMEM_SPEC] * 2,
+        scratch_shapes=[
+            pltpu.VMEM((BD * B, DH), jnp.bfloat16),
+            pltpu.VMEM((BD * B, DH), jnp.bfloat16),
+            dma((n,)), dma((n,)), dma((2,)),
+            dma((2, 2)), dma((2, 2)), dma((2, 2)), dma((2, 2)),
+        ],
+        compiler_params=params(0, 24),
+        name="first",
+    )(row, k, v)
+
+
+TQ = 6
+UN = 8
+W_ANY = 128
+W_ALL = 192
+LFAST = 400
+
+
+def fast_plan_kernel(tab, send_idx, comp, items, last, flag, blk, slot, cells):
+    s, x, z, _ = place()
+    n_home = NX * NZ
+    flags = HD * BD * R
+    for c in range(NX * NZ):
+        cells[c] = 0
+
+    def wipe(i, carry):
+        for h in range(HD):
+            for u in range(4):
+                items[h * LFAST + i * 4 + u] = 0
+        return carry
+
+    lax.fori_loop(0, W_ALL // 4, wipe, 0)
+    for i in range(HD * 64):
+        last[i] = W_ALL
+    for c in range(9):
+        send_idx[c] = 0
+        comp[c] = 0
+
+    def one(home, carry):
+        rank, start = carry
+        zh, xh = home & (NZ - 1), home >> 3
+        start = jnp.where(home == s, rank, start)
+        used = jnp.int32(0)
+        for b in range(BD):
+            k = tab[home, 0, flags + b]
+            col = rank & (NX - 1)
+            cell = cells[col * NZ + zh]
+            mine = (k > 0) & (col == x)
+            at = jnp.where(mine, rank >> 2, 64)
+            blk[at] = home * BD + b
+            slot[at] = zh * 8 + cell
+            comp[jnp.where(mine & (zh == z), cell, 8)] = xh * 2 + used
+            used = used + jnp.where(mine, 1, 0)
+            cells[col * NZ + zh] = cell + k
+            rank = rank + k
+        return rank, start
+
+    total, start = lax.fori_loop(0, n_home, one, (jnp.int32(0), jnp.int32(0)))
+    most = jnp.int32(0)
+    for c in range(NX * NZ):
+        most = jnp.maximum(most, cells[c])
+    flag[0] = jnp.where((total <= 128) & (most <= TQ), 1, 0)
+
+    filled = [jnp.int32(0)] * NX
+    rank = start
+    for j in range(BD):
+        k = tab[s, 0, flags + j]
+        col = rank & (NX - 1)
+        at = jnp.int32(8)
+        for c in range(NX):
+            hit = (k > 0) & (col == c)
+            at = jnp.where(hit, c * 2 + filled[c], at)
+            filled[c] = filled[c] + jnp.where(hit, 1, 0)
+        send_idx[at] = j
+        rank = rank + k
+
+    def query(a, cnt):
+        i = blk[a]
+        home, b = i >> 3, i & (BD - 1)
+        word = slot[a]
+        begin = cnt
+        cnt = list(cnt)
+        lists = [h * LFAST for h in range(HD)]
+
+        def add(h, w, one):
+            items[lists[h] + cnt[h]] = w + jnp.where(cnt[h] == begin[h], 1 << 20, 0)
+            cnt[h] = cnt[h] + one
+
+        for dt in (-1, 0, 1):
+            t = i + dt
+            near = t >> 3
+            ok = (t >= 0) & (t < n_home * BD) & ((near & (NZ - 1)) == z)
+            w = word + (((t >> 6) & 3) * 8 + (t & 7)) * 64
+            one = jnp.where(ok, 1, 0)
+            for h in range(HD):
+                add(h, w, one)
+        one = jnp.where(z == 0, 1, 0)
+        for g in range(G):
+            for h in range(HD):
+                add(h, word + g * 64, one)
+        for h in range(HD):
+            for r in range(R):
+                t = tab[home, 0, h * BD * R + b * R + r]
+                w = word + ((t >> 6) * 8 + (t & 7)) * 64
+                add(h, w, jnp.where(((t >> 3) & (NZ - 1)) == z, 1, 0))
+        for h in range(HD):
+            last[h * 64 + a] = jnp.where(cnt[h] > begin[h], cnt[h] - 1, W_ALL)
+        return tuple(cnt)
+
+    n_mine = (total - x + NX - 1) >> 2
+    cnt = lax.fori_loop(0, n_mine, query, (jnp.int32(0),) * HD)
+    for h in range(HD):
+        items[h * LFAST + cnt[h]] = 0
+
+
+def fast_planned(tab):
+    i32 = lambda n: jax.ShapeDtypeStruct((n,), jnp.int32)
+    return pl.pallas_call(
+        fast_plan_kernel,
+        out_shape=[i32(16), i32(16), i32(HD * LFAST), i32(HD * 64), i32(8)],
+        in_specs=[SMEM_SPEC],
+        out_specs=[SMEM_SPEC] * 5,
+        scratch_shapes=[
+            pltpu.SMEM((72,), jnp.int32),
+            pltpu.SMEM((72,), jnp.int32),
+            pltpu.SMEM((NX * NZ,), jnp.int32),
+        ],
+        compiler_params=params(None, 16),
+        name="fastplan",
+    )(tab)
+
+
+NS = 4
+EXP2 = score_scale * math.log2(math.e)
+Q_UP = [(k, h) for h in range(HD) for k in (1, 2, 3)] + [(4, 0), (4, 2)]
+Q_DOWN = [(k, h) for h in range(HD) for k in (1, 2, 3)] + [(4, 1), (4, 3)]
+M_UP = [(k, h) for h in range(HD) for k in (3, 2, 1)] + [(4, 1), (4, 3)]
+M_DOWN = [(k, h) for h in range(HD) for k in (3, 2, 1)] + [(4, 0), (4, 2)]
+
+
+def main_kernel(idx, comp, items, last, q_any, k_any, v_any, kv_first, out, *rest):
+    kvs, qrs, qzs, cos, cls = rest[0:3], rest[3:7], rest[7:11], rest[11:15], rest[15:19]
+    (qv, kbuf, vbuf, qs, res, rel, st_o, st_m, st_l, mo, ml, ro, rl, fin) = rest[19:33]
+    (load, sqx, rqx, skv, rkv, sfw, rfw, sq, rq, sm, rm, sx, rx) = rest[33:]
+    s, x, z, hd = place()
+    kv_of = (kv_first,) + tuple(kvs)
+
+    def at_x(d):
+        return (lax.rem(x + d, NX) * NZ + z, hd)
+
+    def at_z(d):
+        return (x * NZ + lax.rem(z + d + NZ, NZ), hd)
+
+    def xi(d):
+        return lax.rem(x + d + NX, NX)
+
+    def zi(d):
+        return lax.rem(z + d + NZ, NZ)
+
+    loads = [
+        pltpu.make_async_copy(src, dst, load.at[i])
+        for i, (src, dst) in enumerate(((q_any, qv), (k_any, kbuf), (v_any, vbuf)))
+    ]
+    for copy in loads:
+        copy.start()
+    barrier = pltpu.get_barrier_semaphore()
+    for d in (1, 2, 3):
+        pl.semaphore_signal(barrier, inc=1, device_id=at_x(d), device_id_type=MESH)
+    for d in (1, -1):
+        pl.semaphore_signal(barrier, inc=1, device_id=at_z(d), device_id_type=MESH)
+
+    loads[0].wait()
+
+    def fill(c, carry):
+        col, u = c // 2, lax.rem(c, 2)
+        j = idx[c]
+        for h in range(HD):
+            qs[col, h, u] = qv[j, :, h * DH : (h + 1) * DH]
+        return carry
+
+    lax.fori_loop(0, 8, fill, 0)
+    for h in range(HD):
+        for u in range(2):
+            qrs[h][x, u] = qs[x, h, u]
+    pl.semaphore_wait(barrier, 5)
+
+    sent = []
+
+    def start(copy):
+        copy.start()
+        sent.append(copy)
+
+    def q_move(h, d, src):
+        return pltpu.make_async_remote_copy(
+            src_ref=qs.at[src, h],
+            dst_ref=qrs[h].at[x],
+            send_sem=sqx.at[d, h],
+            recv_sem=rqx.at[d, h],
+            device_id=at_x(d),
+            device_id_type=MESH,
+        )
+
+    for h in range(HD):
+        for d in (1, 3, 2):
+            start(q_move(h, d, xi(d)))
+
+    loads[1].wait()
+    loads[2].wait()
+    gathers = [None]
+    for h in range(1, HD):
+        g = RowGather(kvs[h - 1], (skv.at[h], rkv.at[h], sfw.at[h], rfw.at[h]), x, z, hd)
+        gathers.append(g)
+
+    def prepare(h):
+        def prep(b, carry):
+            rows = pl.ds(pl.multiple_of(b * B, B), B)
+            kvs[h - 1][x, 0, b] = kbuf[rows, h * DH : (h + 1) * DH]
+            kvs[h - 1][x, 1, b] = vbuf[rows, h * DH : (h + 1) * DH].T
+            return carry
+
+        lax.fori_loop(0, BD, prep, 0)
+
+    prepare(1)
+    gathers[1].own()
+
+    def q_copy(up, kk, h, row):
+        n = (Q_UP if up else Q_DOWN).index((kk, h))
+        return pltpu.make_async_remote_copy(
+            src_ref=qzs[h].at[row],
+            dst_ref=qzs[h].at[row],
+            send_sem=sq.at[0 if up else 1, n],
+            recv_sem=rq.at[0 if up else 1, n],
+            device_id=at_z(1 if up else -1),
+            device_id_type=MESH,
+        )
+
+    def q_send(up, kk, h):
+        if (kk, h) in (Q_UP if up else Q_DOWN):
+            start(q_copy(up, kk, h, zi((-1 if up else 1) * (kk - 1))))
+
+    def q_ready(h):
+        for d in (1, 2, 3):
+            src = xi(-d)
+            pltpu.make_async_remote_copy(
+                src_ref=qrs[h].at[src],
+                dst_ref=qrs[h].at[src],
+                send_sem=sqx.at[d, h],
+                recv_sem=rqx.at[d, h],
+                device_id=at_x(d),
+                device_id_type=MESH,
+            ).wait_recv()
+        for c in range(TQ):
+            w = comp[c]
+            qzs[h][z, c] = qrs[h][w >> 1, w & 1]
+
+    def q_begin(h):
+        for up in (True, False):
+            q_send(up, 1, h)
+
+    def q_step(kk, h):
+        for up in (True, False):
+            if (kk, h) in (Q_UP if up else Q_DOWN):
+                q_copy(up, kk, h, zi((-1 if up else 1) * kk)).wait_recv()
+                q_send(up, kk + 1, h)
+
+    nb = jnp.where(z == 0, W_ALL // UN // 4, W_ANY // UN // 4)
+
+    def chunk(h, part):
+        kv, qz = kv_of[h], qzs[h]
+
+        def batch(n, carry):
+            m0, l0, o0 = st_m[...], st_l[...], st_o[...]
+            words = [items[h * LFAST + n * UN + u] for u in range(UN)]
+            scores = []
+            for w in words:
+                spot, tile = w & 63, (w >> 6) & 31
+                scores.append(
+                    lax.dot_general(
+                        kv[tile >> 3, 0, tile & 7],
+                        qz[spot >> 3, spot & 7],
+                        (((1,), (1,)), ((), ())),
+                        preferred_element_type=jnp.float32,
+                    )
+                )
+            tops, weights = [], []
+            for sc in scores:
+                raw = jnp.max(sc, axis=0, keepdims=True)
+                tops.append(raw)
+                weights.append(jnp.exp2((sc - raw) * EXP2).astype(jnp.bfloat16))
+            sums = []
+            for w, p in zip(words, weights):
+                tile = (w >> 6) & 31
+                rows = jnp.concatenate([kv[tile >> 3, 1, tile & 7], ones], axis=0)
+                sums.append(jnp.dot(rows, p, preferred_element_type=jnp.float32))
+            for u, w in enumerate(words):
+                old = jnp.where((w >> 20) > 0, neg_big, m0)
+                top = jnp.maximum(old, tops[u])
+                f0, f1 = jnp.exp2((old - top) * EXP2), jnp.exp2((tops[u] - top) * EXP2)
+                m0 = top
+                l0 = l0 * f0 + sums[u][DH : DH + 1] * f1
+                o0 = o0 * f0 + sums[u][:DH] * f1
+                at = n * UN + u
+                res[at] = o0
+                rel[at] = jnp.concatenate([m0, l0], axis=0)
+            st_m[...], st_l[...], st_o[...] = m0, l0, o0
+            return carry
+
+        ones = jnp.ones((16, B), jnp.bfloat16)
+        lax.fori_loop(part * nb, (part + 1) * nb, batch, 0)
+
+    def collect(h):
+        for a in range(NZ * NS):
+            w = last[h * 64 + a]
+            zp, i = (a >> 1) & 7, (a >> 4) * 2 + (a & 1)
+            l = rel[w, 1:2]
+            cos[h][zp, i] = (res[w] * (1.0 / l)).astype(jnp.bfloat16)
+            cls[h][zp, i] = rel[w, 0:1] * score_scale + jnp.log(l)
+
+    def m_copies(up, kk, h, src_o, src_l):
+        n = (M_UP if up else M_DOWN).index((kk, h))
+        side = 0 if up else 1
+        return [
+            pltpu.make_async_remote_copy(
+                src_ref=src,
+                dst_ref=dst.at[side, n],
+                send_sem=sm.at[i, side, n],
+                recv_sem=rm.at[i, side, n],
+                device_id=at_z(1 if up else -1),
+                device_id_type=MESH,
+            )
+            for i, (src, dst) in enumerate(((src_o, ro), (src_l, rl)))
+        ]
+
+    def m_arrived(up, kk, h):
+        n = (M_UP if up else M_DOWN).index((kk, h))
+        side = 0 if up else 1
+        for copy in m_copies(up, kk, h, ro.at[side, n], rl.at[side, n]):
+            copy.wait_recv()
+        return side, n
+
+    def m_step(kk, h):
+        for up in (True, False):
+            table = M_UP if up else M_DOWN
+            if (kk, h) not in table:
+                continue
+            dest = zi(kk if up else -kk)
+            if (kk + 1, h) not in table:
+                for copy in m_copies(up, kk, h, cos[h].at[dest], cls[h].at[dest]):
+                    start(copy)
+                continue
+            side, prev = m_arrived(up, kk + 1, h)
+            n = table.index((kk, h))
+            for i in range(NS):
+                val, l = merged(cos[h][dest, i], cls[h][dest, i], ro[side, prev, i], rl[side, prev, i])
+                mo[side, n, i] = val.astype(jnp.bfloat16)
+                ml[side, n, i] = l
+            for copy in m_copies(up, kk, h, mo.at[side, n], ml.at[side, n]):
+                start(copy)
+
+    def m_begin(h):
+        collect(h)
+        m_step(4, h)
+        for up in (True, False):
+            table = M_UP if up else M_DOWN
+            if (4, h) not in table:
+                dest = zi(3 if up else -3)
+                for copy in m_copies(up, 3, h, cos[h].at[dest], cls[h].at[dest]):
+                    start(copy)
+
+    def m_second(h):
+        for up in (True, False):
+            table = M_UP if up else M_DOWN
+            if (4, h) in table:
+                dest = zi(3 if up else -3)
+                side, prev = m_arrived(up, 4, h)
+                n = table.index((3, h))
+                for i in range(NS):
+                    val, l = merged(cos[h][dest, i], cls[h][dest, i], ro[side, prev, i], rl[side, prev, i])
+                    mo[side, n, i] = val.astype(jnp.bfloat16)
+                    ml[side, n, i] = l
+                for copy in m_copies(up, 3, h, mo.at[side, n], ml.at[side, n]):
+                    start(copy)
+
+    def final(h, r, d):
+        return pltpu.make_async_remote_copy(
+            src_ref=fin.at[h, r],
+            dst_ref=out.at[:, x, :, h * DH : (h + 1) * DH],
+            send_sem=sx.at[h, r],
+            recv_sem=rx.at[h, d],
+            device_id=(r * NZ + z, hd),
+            device_id_type=MESH,
+        )
+
+    rows = NS // 2
+
+    def m_end(h):
+        su, nu = m_arrived(True, 1, h)
+        sd, nd = m_arrived(False, 1, h)
+        for i in range(NS):
+            a, la = merged(ro[su, nu, i], rl[su, nu, i], ro[sd, nd, i], rl[sd, nd, i])
+            val, _ = merged(cos[h][z, i], cls[h][z, i], a, la)
+            fin[h, i // 2, i % 2] = val.T.astype(jnp.bfloat16)
+        for r in range(rows):
+
+            @pl.when(x == r)
+            def _(r=r):
+                for u in range(2):
+                    out[u, x, :, h * DH : (h + 1) * DH] = fin[h, r, u]
+
+            for d in (1, 2, 3):
+
+                @pl.when(lax.rem(x + d, NX) == r)
+                def _(r=r, d=d):
+                    final(h, r, d).start()
+
+    @pl.when(x >= rows)
+    def _():
+        out[...] = jnp.zeros(out.shape, out.dtype)
+
+    res[W_ALL] = jnp.zeros((DH, B), jnp.float32)
+    rel[W_ALL, 0:1] = jnp.full((1, B), neg_big, jnp.float32)
+    rel[W_ALL, 1:2] = jnp.ones((1, B), jnp.float32)
+    st_o[...] = jnp.zeros((DH, B), jnp.float32)
+    st_m[...] = jnp.full((1, B), neg_big, jnp.float32)
+    st_l[...] = jnp.zeros((1, B), jnp.float32)
+
+    for h in (0, 1):
+        q_ready(h)
+        q_begin(h)
+    prepare(2)
+    prepare(3)
+    q_ready(2)
+    q_ready(3)
+    q_step(1, 0)
+    q_step(1, 1)
+    q_step(2, 0)
+    q_step(2, 1)
+    gathers[1].forward()
+    gathers[2].own()
+    q_step(3, 0)
+    q_step(3, 1)
+    q_begin(2)
+    q_begin(3)
+    q_step(4, 0)
+    chunk(0, 0)
+    q_step(1, 2)
+    chunk(0, 1)
+    q_step(4, 1)
+    q_step(1, 3)
+    chunk(0, 2)
+    gathers[2].forward()
+    gathers[3].own()
+    q_step(2, 2)
+    chunk(0, 3)
+    m_begin(0)
+    q_step(2, 3)
+    gathers[1].finish()
+    chunk(1, 0)
+    q_step(3, 2)
+    chunk(1, 1)
+    q_step(3, 3)
+    m_second(0)
+    chunk(1, 2)
+    q_step(4, 2)
+    q_step(4, 3)
+    chunk(1, 3)
+    m_begin(1)
+    m_step(2, 0)
+    gathers[3].forward()
+    gathers[2].finish()
+    chunk(2, 0)
+    m_second(1)
+    chunk(2, 1)
+    m_step(1, 0)
+    m_step(2, 1)
+    chunk(2, 2)
+    chunk(2, 3)
+    m_begin(2)
+    m_step(1, 1)
+    m_end(0)
+    gathers[3].finish()
+    chunk(3, 0)
+    m_second(2)
+    m_end(1)
+    chunk(3, 1)
+    m_step(2, 2)
+    chunk(3, 2)
+    chunk(3, 3)
+    m_begin(3)
+    m_step(1, 2)
+    m_second(3)
+    m_end(2)
+    m_step(2, 3)
+    m_step(1, 3)
+    m_end(3)
+
+    for h in range(HD):
+        for r in range(rows):
+
+            @pl.when(x == r)
+            def _(h=h, r=r):
+                for d in (1, 2, 3):
+                    src = lax.rem(x - d + NX, NX)
+                    pltpu.make_async_remote_copy(
+                        src_ref=fin.at[h, r],
+                        dst_ref=out.at[:, src, :, h * DH : (h + 1) * DH],
+                        send_sem=sx.at[h, r],
+                        recv_sem=rx.at[h, d],
+                        device_id=at_x(d),
+                        device_id_type=MESH,
+                    ).wait_recv()
+
+            for d in (1, 2, 3):
+
+                @pl.when(lax.rem(x + d, NX) == r)
+                def _(h=h, r=r, d=d):
+                    final(h, r, d).wait_send()
+
+    for g in gathers[1:]:
+        g.close()
+    for copy in sent:
+        copy.wait_send()
+
+
+def main_step(idx, comp, items, last, q, k, v, kv_first):
+    dma = pltpu.SemaphoreType.DMA
+    any_spec = pl.BlockSpec(memory_space=pl.ANY)
+    bf, f32 = jnp.bfloat16, jnp.float32
+    out = pl.pallas_call(
+        main_kernel,
+        out_shape=jax.ShapeDtypeStruct((2, NX, B, HD * DH), bf),
+        in_specs=[SMEM_SPEC] * 4 + [any_spec] * 3 + [VMEM_SPEC],
         out_specs=VMEM_SPEC,
-        scratch_shapes=[pltpu.SemaphoreType.DMA((n,)), pltpu.SemaphoreType.DMA((n,))],
-        compiler_params=params(0, 16),
-        name="table",
-    )(row)
+        scratch_shapes=[pltpu.VMEM((NX, 2, BD, B, DH), bf)] * 3
+        + [pltpu.VMEM((NX, 2, B, DH), bf)] * HD
+        + [pltpu.VMEM((NZ, TQ, B, DH), bf)] * HD
+        + [pltpu.VMEM((NZ, NS, DH, B), bf)] * HD
+        + [pltpu.VMEM((NZ, NS, 1, B), f32)] * HD
+        + [
+            pltpu.VMEM((BD, B, HD * DH), bf),
+            pltpu.VMEM((BD * B, HD * DH), bf),
+            pltpu.VMEM((BD * B, HD * DH), bf),
+            pltpu.VMEM((NX, HD, 2, B, DH), bf),
+            pltpu.VMEM((W_ALL + 1, DH, B), f32),
+            pltpu.VMEM((W_ALL + 1, 2, B), f32),
+            pltpu.VMEM((DH, B), f32),
+            pltpu.VMEM((1, B), f32),
+            pltpu.VMEM((1, B), f32),
+            pltpu.VMEM((2, 14, NS, DH, B), bf),
+            pltpu.VMEM((2, 14, NS, 1, B), f32),
+            pltpu.VMEM((2, 14, NS, DH, B), bf),
+            pltpu.VMEM((2, 14, NS, 1, B), f32),
+            pltpu.VMEM((HD, NS // 2, 2, B, DH), bf),
+        ]
+        + [
+            dma((3,)),
+            dma((4, HD)), dma((4, HD)),
+            dma((HD, 2, 2)), dma((HD, 2, 2)), dma((HD, 2, 2)), dma((HD, 2, 2)),
+            dma((2, 14)), dma((2, 14)),
+            dma((2, 2, 14)), dma((2, 2, 14)),
+            dma((HD, NS // 2)), dma((HD, 4)),
+        ],
+        compiler_params=params(1, 58),
+        name="main",
+    )(idx, comp, items, last, q, k, v, kv_first)
+    return out.reshape(BD * B, HD * DH)
 
 
 def plan_kernel(tab, send_idx, items, counts, blk, slot):
@@ -359,7 +994,7 @@
             dma((14,)),
             dma((14,)),
         ],
-        compiler_params=params(1),
+        compiler_params=params(2),
         name="spread",
     )(idx, q, k, v)
 
@@ -618,7 +1253,7 @@
             dma((2, 14)), dma((2, 14)), dma((2, 14)), dma((2, 14)),
             dma((4,)), dma((4,)),
         ],
-        compiler_params=params(2 + ns // 8, 56),
+        compiler_params=params(3, 56),
         name="join%d" % ns,
     )(o, lse)
     return out.reshape(BD * B, HD * DH)
@@ -627,18 +1262,21 @@
 def body(queries, keys, values, random_holder, random_offset, keep):
     want = random_holder * BD + random_offset
     row = jnp.concatenate([want.reshape(-1), keep, jnp.zeros((24,), jnp.int32)])
-    tab = gathered_table(row.reshape(1, 128))
-    total = jnp.sum(tab[:, 0, HD * BD * R : HD * BD * R + BD])
-    send_idx, items, counts = planned(tab)
-    kv, qz = spread_all(send_idx, queries.reshape(BD, B, HD * DH), keys, values)
-
-    def tail(ns):
-        def run(items, counts, kv, qz):
-            return joined(ns, *parts_of(ns, items, counts, kv, qz))
-
-        return run
-
-    return lax.cond(total <= 128, tail(4), tail(8), items, counts, kv, qz)
+    tab, kv_first = first_step(row.reshape(1, 128), keys, values)
+    q = queries.reshape(BD, B, HD * DH)
+    idx, comp, items, last, flag = fast_planned(tab)
+
+    def fast(idx, comp, items, last, tab, q, keys, values, kv_first):
+        return main_step(idx, comp, items, last, q, keys, values, kv_first)
+
+    def wide(idx, comp, items, last, tab, q, keys, values, kv_first):
+        send_idx, items, counts = planned(tab)
+        kv, qz = spread_all(send_idx, q, keys, values)
+        return joined(8, *parts_of(8, items, counts, kv, qz))
+
+    return lax.cond(
+        flag[0] > 0, fast, wide, idx, comp, items, last, tab, q, keys, values, kv_first
+    )
 
 
 def solution(mesh):

time: 280 us -> 175 us (0.62)
  Pallas kernels: 270 us -> 172 us
  local copies, waits for them, and re-layouts: 7.44 us -> 1.18 us
    pallas_call x5 -> x3, Pallas kernels: 270 us -> 172 us  [the longest x1 133 us: main_step(): pl.pallas_call(main_kernel, out_shape=jax.ShapeDtypeStruct((2, NX, B, HD...]
    unnamed x7 -> x1, local copies, waits for them, and re-layouts: 4.64 us -> 0.97 us
where the time goes in v2:
time: 175 us; the launch traced here: 174 us
  Pallas kernels  172 us (98%)
    pallas_call x1, Pallas kernels, main_step(): pl.pallas_call(main_kernel, out_shape=jax.ShapeDtypeStruct((2, NX, B, HD...  133 us
    pallas_call x1, Pallas kernels, first_step(): pl.pallas_call(first_kernel, out_shape=[jax.ShapeDtypeStruct((n, 1, 128),...  29.3 us
    pallas_call x1, Pallas kernels, fast_planned(): pl.pallas_call(fast_plan_kernel, out_shape=[i32(16), i32(16), i32(HD * LF...  8.85 us

profile of v2, /device:TPU:24, one launch (start us, length us, event | category | flops | bytes accessed | tf_op | source)
XLA Modules:
  0.0 174.4 jit_solution(1816336484961760260)
XLA Ops:
  0.0 0.7 multiply_add_fusion
  0.7 0.1 copy.10
  0.8 0.1 reshape.19
  0.9 0.7 add_bitcast_fusion.row
  1.7 29.3 %first.1 = (s32[32,1,128]{2,1,0:T(1,128)S(1)}, bf16[4,2,8,128,128]{4,3,2,1,0:T(8,128)(2,1)S(1)}) custom-call(s32[1,128]{1,0:T(1,128)S(1)} %add_bitcast_fusion.row, bf16[1024,512]{1,0:T(8,128)(2,1)} %k.1, bf16[1024,512]{1,0:T(8,128)(2,1)} %v.1), custom_call_target="tpu_custom_call" | custom-call | tf_op jit(solution)/shard_map/first/pallas_call | solution.py:143
  31.0 8.9 %fastplan.1 = (s32[16]{0:T(128)S(1)}, s32[16]{0:T(128)S(1)}, s32[1600]{0:T(1024)S(1)}, s32[256]{0:T(256)S(1)}, s32[8]{0:T(128)S(1)}) custom-call(s32[32,1,128]{2,1,0:T(1,128)S(1)} %get-tuple-element.58.tab), custom_call_target="tpu_custom_call" | custom-call | tf_op jit(solution)/shard_map/fastplan/pallas_call | solution.py:268
  39.9 133.5 %conditional.1 = (bf16[1024,512]{1,0:T(8,128)(2,1)S(1)}) conditional(s32[]{:T(128)} %bitcast.3, (s32[32,1,128]{2,1,0:T(1,128)S(1)}, bf16[8,128,512]{2,1,0:T(8,128)(2,1)}, bf16[1024,512]{1,0:T(8,128)(2,1)}, bf16[1024,512]{1,0:T(8,128)(2,1)}) %tuple.17, (s32[16]{0:T(128)S(1)}, s32[16]{0:T(128)S(1)}, s32[1600]{0:T(1024)S(1)}, s32[256]{0:T(256)S(1)}, ...), branch_computations={%region_0.0_spmd, %region_1.0_spmd} | conditional | bytes 34078784 | solution.py:1277
  39.9 133.3 %main.1 = bf16[2,4,128,512]{3,2,1,0:T(8,128)(2,1)S(1)} custom-call(s32[16]{0:T(128)S(1)} %get-tuple-element.43.idx, s32[16]{0:T(128)S(1)} %get-tuple-element.44.comp, s32[1600]{0:T(1024)S(1)} %get-tuple-element.45.items, s32[256]{0:T(256)S(1)} %get-tuple-element.46.last, bf16[8,128,512]{2,1,0:T(8,128)(2,1)} %get-tuple-element.47.q_any, ...), custom_call_target="tpu_custom_call" | custom-call | tf_op jit(solution)/shard_map/cond/branch_1_fun/main/pallas_call | solution.py:679
  173.5 1.0 copy.14
  (1 shorter events, 0.0 us)

commit v3 on v2

--- a/solution.py
+++ b/solution.py
@@ -42,31 +42,15 @@
     )
 
 
-def first_kernel(row, k, v, tab, kv, ks, vs, send_sem, recv_sem, load, sk, rk, sf, rf):
-    s, x, z, hd = place()
+def table_kernel(row, tab, send_sem, recv_sem):
+    s, _, _, h = place()
     n = NX * NZ
-    loads = [
-        pltpu.make_async_copy(k.at[:, :DH], ks, load.at[0]),
-        pltpu.make_async_copy(v.at[:, :DH], vs, load.at[1]),
-    ]
-    for copy in loads:
-        copy.start()
     barrier = pltpu.get_barrier_semaphore()
     for d in range(1, n):
         pl.semaphore_signal(
-            barrier, inc=1, device_id=(lax.rem(s + d, n), hd), device_id_type=MESH
+            barrier, inc=1, device_id=(lax.rem(s + d, n), h), device_id_type=MESH
         )
     tab[s] = row[...]
-    for copy in loads:
-        copy.wait()
-
-    def prep(b, carry):
-        rows = pl.ds(pl.multiple_of(b * B, B), B)
-        kv[x, 0, b] = ks[rows, :]
-        kv[x, 1, b] = vs[rows, :].T
-        return carry
-
-    lax.fori_loop(0, BD, prep, 0)
     pl.semaphore_wait(barrier, n - 1)
     copies = []
     for d in range(1, n):
@@ -75,19 +59,26 @@
             dst_ref=tab.at[s],
             send_sem=send_sem.at[d],
             recv_sem=recv_sem.at[d],
-            device_id=(lax.rem(s + d, n), hd),
+            device_id=(lax.rem(s + d, n), h),
             device_id_type=MESH,
         )
         copy.start()
         copies.append(copy)
-
-    gather = RowGather(kv, (sk, rk, sf, rf), x, z, hd)
-    gather.own()
-    gather.forward()
-    gather.finish()
     for copy in copies:
         copy.wait()
-    gather.close()
+
+
+def gathered_table(row):
+    n = NX * NZ
+    return pl.pallas_call(
+        table_kernel,
+        out_shape=jax.ShapeDtypeStruct((n, 1, 128), jnp.int32),
+        in_specs=[VMEM_SPEC],
+        out_specs=VMEM_SPEC,
+        scratch_shapes=[pltpu.SemaphoreType.DMA((n,)), pltpu.SemaphoreType.DMA((n,))],
+        compiler_params=params(0, 16),
+        name="table",
+    )(row)
 
 
 class RowGather:
@@ -136,52 +127,50 @@
             copy.wait_send()
 
 
-def first_step(row, k, v):
-    n = NX * NZ
-    dma = pltpu.SemaphoreType.DMA
-    any_spec = pl.BlockSpec(memory_space=pl.ANY)
-    return pl.pallas_call(
-        first_kernel,
-        out_shape=[
-            jax.ShapeDtypeStruct((n, 1, 128), jnp.int32),
-            jax.ShapeDtypeStruct((NX, 2, BD, B, DH), jnp.bfloat16),
-        ],
-        in_specs=[VMEM_SPEC, any_spec, any_spec],
-        out_specs=[VMEM_SPEC] * 2,
-        scratch_shapes=[
-            pltpu.VMEM((BD * B, DH), jnp.bfloat16),
-            pltpu.VMEM((BD * B, DH), jnp.bfloat16),
-            dma((n,)), dma((n,)), dma((2,)),
-            dma((2, 2)), dma((2, 2)), dma((2, 2)), dma((2, 2)),
-        ],
-        compiler_params=params(0, 24),
-        name="first",
-    )(row, k, v)
-
-
-TQ = 6
 UN = 8
 W_ANY = 128
 W_ALL = 192
 LFAST = 400
 
 
-def fast_plan_kernel(tab, send_idx, comp, items, last, flag, blk, slot, cells):
+def fast_plan_kernel(tab, tabv, send_idx, comp, items, last, flag, blk, slot, cells):
     s, x, z, _ = place()
     n_home = NX * NZ
     flags = HD * BD * R
-    for c in range(NX * NZ):
+
+    lane = lax.broadcasted_iota(jnp.int32, (n_home, 128), 1)
+    kept = jnp.where((lane >= flags) & (lane < flags + BD), tabv[:, 0, :], 0).astype(jnp.float32)
+    before = (
+        lax.broadcasted_iota(jnp.int32, (128, 128), 0)
+        < lax.broadcasted_iota(jnp.int32, (128, 128), 1)
+    ).astype(jnp.float32)
+    above = (
+        lax.broadcasted_iota(jnp.int32, (n_home, n_home), 1)
+        < lax.broadcasted_iota(jnp.int32, (n_home, n_home), 0)
+    ).astype(jnp.float32)
+    in_row = jnp.dot(kept, before, preferred_element_type=jnp.float32)
+    rows = jnp.sum(kept, axis=1, keepdims=True)
+    upper = jnp.dot(above, jnp.broadcast_to(rows, (n_home, 128)), preferred_element_type=jnp.float32)
+    ranks = (in_row + upper).astype(jnp.int32)
+    most = jnp.zeros((NZ, 1), jnp.float32)
+    for c in range(NX):
+        n = jnp.sum(jnp.where((ranks & (NX - 1)) == c, kept, 0.0), axis=1, keepdims=True)
+        most = jnp.maximum(most, n[0:8] + n[8:16] + n[16:24] + n[24:32])
+    most = jnp.max(most)
+
+    for c in range(NZ):
         cells[c] = 0
 
     def wipe(i, carry):
         for h in range(HD):
-            for u in range(4):
-                items[h * LFAST + i * 4 + u] = 0
+            for u in range(8):
+                items[h * LFAST + i * 8 + u] = 0
         return carry
 
-    lax.fori_loop(0, W_ALL // 4, wipe, 0)
-    for i in range(HD * 64):
-        last[i] = W_ALL
+    lax.fori_loop(0, W_ALL // 8, wipe, 0)
+    for h in range(HD):
+        for i in range(32):
+            last[h * 64 + i] = W_ALL
     for c in range(9):
         send_idx[c] = 0
         comp[c] = 0
@@ -190,26 +179,26 @@
         rank, start = carry
         zh, xh = home & (NZ - 1), home >> 3
         start = jnp.where(home == s, rank, start)
-        used = jnp.int32(0)
+        used = xh * 2
+        cell = cells[zh]
+        here = zh == z
         for b in range(BD):
             k = tab[home, 0, flags + b]
-            col = rank & (NX - 1)
-            cell = cells[col * NZ + zh]
-            mine = (k > 0) & (col == x)
+            mine = (k > 0) & ((rank & (NX - 1)) == x)
             at = jnp.where(mine, rank >> 2, 64)
             blk[at] = home * BD + b
             slot[at] = zh * 8 + cell
-            comp[jnp.where(mine & (zh == z), cell, 8)] = xh * 2 + used
-            used = used + jnp.where(mine, 1, 0)
-            cells[col * NZ + zh] = cell + k
+            comp[jnp.where(mine & here, cell, 8)] = used
+            add = jnp.where(mine, 1, 0)
+            used = used + add
+            cell = cell + add
             rank = rank + k
+        cells[zh] = cell
         return rank, start
 
     total, start = lax.fori_loop(0, n_home, one, (jnp.int32(0), jnp.int32(0)))
-    most = jnp.int32(0)
-    for c in range(NX * NZ):
-        most = jnp.maximum(most, cells[c])
-    flag[0] = jnp.where((total <= 128) & (most <= TQ), 1, 0)
+    fits = jnp.where(most <= 5.0, 2, jnp.where(most <= 6.0, 1, 0))
+    flag[0] = jnp.where(total <= 128, fits, 0)
 
     filled = [jnp.int32(0)] * NX
     rank = start
@@ -228,12 +217,11 @@
         i = blk[a]
         home, b = i >> 3, i & (BD - 1)
         word = slot[a]
-        begin = cnt
-        cnt = list(cnt)
-        lists = [h * LFAST for h in range(HD)]
+        begin = [c + h * LFAST for h, c in enumerate(cnt)]
+        cnt = list(begin)
 
         def add(h, w, one):
-            items[lists[h] + cnt[h]] = w + jnp.where(cnt[h] == begin[h], 1 << 20, 0)
+            items[cnt[h]] = w + jnp.where(cnt[h] == begin[h], 1 << 20, 0)
             cnt[h] = cnt[h] + one
 
         for dt in (-1, 0, 1):
@@ -244,18 +232,24 @@
             one = jnp.where(ok, 1, 0)
             for h in range(HD):
                 add(h, w, one)
-        one = jnp.where(z == 0, 1, 0)
-        for g in range(G):
-            for h in range(HD):
-                add(h, word + g * 64, one)
         for h in range(HD):
             for r in range(R):
                 t = tab[home, 0, h * BD * R + b * R + r]
                 w = word + ((t >> 6) * 8 + (t & 7)) * 64
                 add(h, w, jnp.where(((t >> 3) & (NZ - 1)) == z, 1, 0))
+
+        def with_shared(*cnt):
+            cnt = list(cnt)
+            for h in range(HD):
+                for g in range(G):
+                    items[cnt[h]] = word + g * 64 + jnp.where(cnt[h] == begin[h], 1 << 20, 0)
+                    cnt[h] = cnt[h] + 1
+            return tuple(cnt)
+
+        cnt = lax.cond(z == 0, with_shared, lambda *cnt: tuple(cnt), *cnt)
         for h in range(HD):
-            last[h * 64 + a] = jnp.where(cnt[h] > begin[h], cnt[h] - 1, W_ALL)
-        return tuple(cnt)
+            last[h * 64 + a] = jnp.where(cnt[h] > begin[h], cnt[h] - 1 - h * LFAST, W_ALL)
+        return tuple(c - h * LFAST for h, c in enumerate(cnt))
 
     n_mine = (total - x + NX - 1) >> 2
     cnt = lax.fori_loop(0, n_mine, query, (jnp.int32(0),) * HD)
@@ -268,16 +262,16 @@
     return pl.pallas_call(
         fast_plan_kernel,
         out_shape=[i32(16), i32(16), i32(HD * LFAST), i32(HD * 64), i32(8)],
-        in_specs=[SMEM_SPEC],
+        in_specs=[SMEM_SPEC, VMEM_SPEC],
         out_specs=[SMEM_SPEC] * 5,
         scratch_shapes=[
             pltpu.SMEM((72,), jnp.int32),
             pltpu.SMEM((72,), jnp.int32),
-            pltpu.SMEM((NX * NZ,), jnp.int32),
+            pltpu.SMEM((NZ,), jnp.int32),
         ],
         compiler_params=params(None, 16),
         name="fastplan",
-    )(tab)
+    )(tab, tab)
 
 
 NS = 4
@@ -288,12 +282,11 @@
 M_DOWN = [(k, h) for h in range(HD) for k in (3, 2, 1)] + [(4, 0), (4, 2)]
 
 
-def main_kernel(idx, comp, items, last, q_any, k_any, v_any, kv_first, out, *rest):
-    kvs, qrs, qzs, cos, cls = rest[0:3], rest[3:7], rest[7:11], rest[11:15], rest[15:19]
-    (qv, kbuf, vbuf, qs, res, rel, st_o, st_m, st_l, mo, ml, ro, rl, fin) = rest[19:33]
-    (load, sqx, rqx, skv, rkv, sfw, rfw, sq, rq, sm, rm, sx, rx) = rest[33:]
+def main_kernel(tq, idx, comp, items, last, q_any, k_any, v_any, out, *rest):
+    kvs, qrs, qzs, cos, cls = rest[0:4], rest[4:8], rest[8:12], rest[12:16], rest[16:20]
+    (qv, kbuf, vbuf, qs, res, rel, st_o, st_m, st_l, mo, ml, ro, rl, fin) = rest[20:34]
+    (load, sqx, rqx, skv, rkv, sfw, rfw, sq, rq, sm, rm, sx, rx) = rest[34:]
     s, x, z, hd = place()
-    kv_of = (kv_first,) + tuple(kvs)
 
     def at_x(d):
         return (lax.rem(x + d, NX) * NZ + z, hd)
@@ -356,22 +349,22 @@
 
     loads[1].wait()
     loads[2].wait()
-    gathers = [None]
-    for h in range(1, HD):
-        g = RowGather(kvs[h - 1], (skv.at[h], rkv.at[h], sfw.at[h], rfw.at[h]), x, z, hd)
+    gathers = []
+    for h in range(HD):
+        g = RowGather(kvs[h], (skv.at[h], rkv.at[h], sfw.at[h], rfw.at[h]), x, z, hd)
         gathers.append(g)
 
     def prepare(h):
         def prep(b, carry):
             rows = pl.ds(pl.multiple_of(b * B, B), B)
-            kvs[h - 1][x, 0, b] = kbuf[rows, h * DH : (h + 1) * DH]
-            kvs[h - 1][x, 1, b] = vbuf[rows, h * DH : (h + 1) * DH].T
+            kvs[h][x, 0, b] = kbuf[rows, h * DH : (h + 1) * DH]
+            kvs[h][x, 1, b] = vbuf[rows, h * DH : (h + 1) * DH].T
             return carry
 
         lax.fori_loop(0, BD, prep, 0)
 
-    prepare(1)
-    gathers[1].own()
+    prepare(0)
+    gathers[0].own()
 
     def q_copy(up, kk, h, row):
         n = (Q_UP if up else Q_DOWN).index((kk, h))
@@ -399,7 +392,7 @@
                 device_id=at_x(d),
                 device_id_type=MESH,
             ).wait_recv()
-        for c in range(TQ):
+        for c in range(tq):
             w = comp[c]
             qzs[h][z, c] = qrs[h][w >> 1, w & 1]
 
@@ -416,7 +409,7 @@
     nb = jnp.where(z == 0, W_ALL // UN // 4, W_ANY // UN // 4)
 
     def chunk(h, part):
-        kv, qz = kv_of[h], qzs[h]
+        kv, qz = kvs[h], qzs[h]
 
         def batch(n, carry):
             m0, l0, o0 = st_m[...], st_l[...], st_o[...]
@@ -577,29 +570,31 @@
     for h in (0, 1):
         q_ready(h)
         q_begin(h)
-    prepare(2)
-    prepare(3)
+    prepare(1)
     q_ready(2)
     q_ready(3)
     q_step(1, 0)
     q_step(1, 1)
+    gathers[0].forward()
+    gathers[1].own()
+    prepare(2)
+    prepare(3)
     q_step(2, 0)
     q_step(2, 1)
-    gathers[1].forward()
-    gathers[2].own()
     q_step(3, 0)
     q_step(3, 1)
     q_begin(2)
     q_begin(3)
     q_step(4, 0)
+    gathers[0].finish()
     chunk(0, 0)
     q_step(1, 2)
     chunk(0, 1)
     q_step(4, 1)
+    gathers[1].forward()
+    gathers[2].own()
     q_step(1, 3)
     chunk(0, 2)
-    gathers[2].forward()
-    gathers[3].own()
     q_step(2, 2)
     chunk(0, 3)
     m_begin(0)
@@ -608,6 +603,8 @@
     chunk(1, 0)
     q_step(3, 2)
     chunk(1, 1)
+    gathers[2].forward()
+    gathers[3].own()
     q_step(3, 3)
     m_second(0)
     chunk(1, 2)
@@ -616,11 +613,11 @@
     chunk(1, 3)
     m_begin(1)
     m_step(2, 0)
-    gathers[3].forward()
     gathers[2].finish()
     chunk(2, 0)
     m_second(1)
     chunk(2, 1)
+    gathers[3].forward()
     m_step(1, 0)
     m_step(2, 1)
     chunk(2, 2)
@@ -666,24 +663,24 @@
                 def _(h=h, r=r, d=d):
                     final(h, r, d).wait_send()
 
-    for g in gathers[1:]:
+    for g in gathers:
         g.close()
     for copy in sent:
         copy.wait_send()
 
 
-def main_step(idx, comp, items, last, q, k, v, kv_first):
+def main_step(tq, idx, comp, items, last, q, k, v):
     dma = pltpu.SemaphoreType.DMA
     any_spec = pl.BlockSpec(memory_space=pl.ANY)
     bf, f32 = jnp.bfloat16, jnp.float32
     out = pl.pallas_call(
-        main_kernel,
+        functools.partial(main_kernel, tq),
         out_shape=jax.ShapeDtypeStruct((2, NX, B, HD * DH), bf),
-        in_specs=[SMEM_SPEC] * 4 + [any_spec] * 3 + [VMEM_SPEC],
+        in_specs=[SMEM_SPEC] * 4 + [any_spec] * 3,
         out_specs=VMEM_SPEC,
-        scratch_shapes=[pltpu.VMEM((NX, 2, BD, B, DH), bf)] * 3
+        scratch_shapes=[pltpu.VMEM((NX, 2, BD, B, DH), bf)] * HD
         + [pltpu.VMEM((NX, 2, B, DH), bf)] * HD
-        + [pltpu.VMEM((NZ, TQ, B, DH), bf)] * HD
+        + [pltpu.VMEM((NZ, tq, B, DH), bf)] * HD
         + [pltpu.VMEM((NZ, NS, DH, B), bf)] * HD
         + [pltpu.VMEM((NZ, NS, 1, B), f32)] * HD
         + [
@@ -710,9 +707,9 @@
             dma((2, 2, 14)), dma((2, 2, 14)),
             dma((HD, NS // 2)), dma((HD, 4)),
         ],
-        compiler_params=params(1, 58),
-        name="main",
-    )(idx, comp, items, last, q, k, v, kv_first)
+        compiler_params=params(tq, 58),
+        name="main%d" % tq,
+    )(idx, comp, items, last, q, k, v)
     return out.reshape(BD * B, HD * DH)
 
 
@@ -1262,20 +1259,23 @@
 def body(queries, keys, values, random_holder, random_offset, keep):
     want = random_holder * BD + random_offset
     row = jnp.concatenate([want.reshape(-1), keep, jnp.zeros((24,), jnp.int32)])
-    tab, kv_first = first_step(row.reshape(1, 128), keys, values)
+    tab = gathered_table(row.reshape(1, 128))
     q = queries.reshape(BD, B, HD * DH)
     idx, comp, items, last, flag = fast_planned(tab)
 
-    def fast(idx, comp, items, last, tab, q, keys, values, kv_first):
-        return main_step(idx, comp, items, last, q, keys, values, kv_first)
-
-    def wide(idx, comp, items, last, tab, q, keys, values, kv_first):
+    def fast(tq):
+        def run(idx, comp, items, last, tab, q, keys, values):
+            return main_step(tq, idx, comp, items, last, q, keys, values)
+
+        return run
+
+    def wide(idx, comp, items, last, tab, q, keys, values):
         send_idx, items, counts = planned(tab)
         kv, qz = spread_all(send_idx, q, keys, values)
         return joined(8, *parts_of(8, items, counts, kv, qz))
 
-    return lax.cond(
-        flag[0] > 0, fast, wide, idx, comp, items, last, tab, q, keys, values, kv_first
+    return lax.switch(
+        flag[0], (wide, fast(6), fast(5)), idx, comp, items, last, tab, q, keys, values
     )
 
 

time: 175 us -> 162 us (0.926)
  Pallas kernels: 172 us -> 159 us
    pallas_call x2, Pallas kernels: 163 us -> 149 us  [the longest x1 134 us: main_step(): pl.pallas_call(functools.partial(main_kernel, tq), out_shape=jax.ShapeDty...]
where the time goes in v3:
time: 162 us
  Pallas kernels  159 us (98%)
    pallas_call x1, Pallas kernels, main_step(): pl.pallas_call(functools.partial(main_kernel, tq), out_shape=jax.ShapeDty...  134 us
    pallas_call x1, Pallas kernels, gathered_table(): pl.pallas_call(table_kernel, out_shape=jax.ShapeDtypeStruct((n, 1, 128),...  14.7 us
    pallas_call x1, Pallas kernels, fast_planned(): pl.pallas_call(fast_plan_kernel, out_shape=[i32(16), i32(16), i32(HD * LF...  9.54 us

profile of v3, /device:TPU:24, one launch (start us, length us, event | category | flops | bytes accessed | tf_op | source)
XLA Modules:
  0.0 161.9 jit_solution(14373952744967345238)
XLA Ops:
  0.0 0.7 multiply_add_fusion
  0.7 0.1 copy.11
  0.8 0.1 reshape.21
  0.9 0.7 add_bitcast_fusion.row
  1.7 14.7 %table.1.tab.tabv = s32[32,1,128]{2,1,0:T(1,128)S(1)} custom-call(s32[1,128]{1,0:T(1,128)S(1)} %add_bitcast_fusion.row), custom_call_target="tpu_custom_call" | custom-call | tf_op jit(solution)/shard_map/table/pallas_call | solution.py:73
  16.4 9.5 %fastplan.1 = (s32[16]{0:T(128)S(1)}, s32[16]{0:T(128)S(1)}, s32[1600]{0:T(1024)S(1)}, s32[256]{0:T(256)S(1)}, s32[8]{0:T(128)S(1)}) custom-call(s32[32,1,128]{2,1,0:T(1,128)S(1)} %table.1.tab.tabv, s32[32,1,128]{2,1,0:T(1,128)S(1)} %table.1.tab.tabv), custom_call_target="tpu_custom_call" | custom-call | tf_op jit(solution)/shard_map/fastplan/pallas_call | solution.py:262
  26.0 134.9 %conditional.1 = (bf16[1024,512]{1,0:T(8,128)(2,1)S(1)}) conditional(s32[]{:T(128)} %bitcast.4, (s32[32,1,128]{2,1,0:T(1,128)S(1)}, bf16[8,128,512]{2,1,0:T(8,128)(2,1)}, bf16[1024,512]{1,0:T(8,128)(2,1)}, bf16[1024,512]{1,0:T(8,128)(2,1)}) %tuple.22, (s32[16]{0:T(128)S(1)}, s32[16]{0:T(128)S(1)}, s32[1600]{0:T(1024)S(1)}, ...), branch_computations={%region_0.0_spmd, %region_1.0_spmd, %region_2.0_spmd} | conditional | bytes 34078784 | solution.py:1277
  26.0 134.4 %main6.1 = bf16[2,4,128,512]{3,2,1,0:T(8,128)(2,1)S(1)} custom-call(s32[16]{0:T(128)S(1)} %get-tuple-element.56.idx, s32[16]{0:T(128)S(1)} %get-tuple-element.57.comp, s32[1600]{0:T(1024)S(1)} %get-tuple-element.58.items, s32[256]{0:T(256)S(1)} %get-tuple-element.59.last, bf16[8,128,512]{2,1,0:T(8,128)(2,1)} %get-tuple-element.60.q_any, ...), custom_call_target="tpu_custom_call" | custom-call | tf_op jit(solution)/shard_map/cond/branch_1_fun/main6/pallas_call | solution.py:676
  160.9 1.0 copy.16
  (1 shorter events, 0.0 us)

commit v4 on v3

--- a/solution.py
+++ b/solution.py
@@ -1,4 +1,3 @@
-import functools
 import math
 
 import jax
@@ -16,7 +15,12 @@
 NZ = 8
 HD = 4
 BD = 8
-LCAP = 400
+TQ = 6
+NS = 4
+UN = 8
+W_ANY = 128
+W_ALL = 192
+STEP = 32 * NX
 
 neg_big = -1e30
 MESH = pl.DeviceIdType.MESH
@@ -40,45 +44,6 @@
     return pltpu.CompilerParams(
         collective_id=cid, has_side_effects=True, vmem_limit_bytes=mib << 20
     )
-
-
-def table_kernel(row, tab, send_sem, recv_sem):
-    s, _, _, h = place()
-    n = NX * NZ
-    barrier = pltpu.get_barrier_semaphore()
-    for d in range(1, n):
-        pl.semaphore_signal(
-            barrier, inc=1, device_id=(lax.rem(s + d, n), h), device_id_type=MESH
-        )
-    tab[s] = row[...]
-    pl.semaphore_wait(barrier, n - 1)
-    copies = []
-    for d in range(1, n):
-        copy = pltpu.make_async_remote_copy(
-            src_ref=row,
-            dst_ref=tab.at[s],
-            send_sem=send_sem.at[d],
-            recv_sem=recv_sem.at[d],
-            device_id=(lax.rem(s + d, n), h),
-            device_id_type=MESH,
-        )
-        copy.start()
-        copies.append(copy)
-    for copy in copies:
-        copy.wait()
-
-
-def gathered_table(row):
-    n = NX * NZ
-    return pl.pallas_call(
-        table_kernel,
-        out_shape=jax.ShapeDtypeStruct((n, 1, 128), jnp.int32),
-        in_specs=[VMEM_SPEC],
-        out_specs=VMEM_SPEC,
-        scratch_shapes=[pltpu.SemaphoreType.DMA((n,)), pltpu.SemaphoreType.DMA((n,))],
-        compiler_params=params(0, 16),
-        name="table",
-    )(row)
 
 
 class RowGather:
@@ -127,154 +92,121 @@
             copy.wait_send()
 
 
-UN = 8
-W_ANY = 128
-W_ALL = 192
-LFAST = 400
-
-
-def fast_plan_kernel(tab, tabv, send_idx, comp, items, last, flag, blk, slot, cells):
-    s, x, z, _ = place()
-    n_home = NX * NZ
+def merged(o0, l0, o1, l1):
+    top = jnp.maximum(l0, l1)
+    f0, f1 = jnp.exp(l0 - top), jnp.exp(l1 - top)
+    both = f0 + f1
+    o = (o0.astype(jnp.float32) * f0 + o1.astype(jnp.float32) * f1) / both
+    return o, top + jnp.log(both)
+
+
+def plan(tab, window, part, s, x, z, sendm, lastm, itemm, info):
+    n_home, wide = NX * NZ, 128
     flags = HD * BD * R
-
-    lane = lax.broadcasted_iota(jnp.int32, (n_home, 128), 1)
-    kept = jnp.where((lane >= flags) & (lane < flags + BD), tabv[:, 0, :], 0).astype(jnp.float32)
-    before = (
-        lax.broadcasted_iota(jnp.int32, (128, 128), 0)
-        < lax.broadcasted_iota(jnp.int32, (128, 128), 1)
-    ).astype(jnp.float32)
-    above = (
-        lax.broadcasted_iota(jnp.int32, (n_home, n_home), 1)
-        < lax.broadcasted_iota(jnp.int32, (n_home, n_home), 0)
-    ).astype(jnp.float32)
-    in_row = jnp.dot(kept, before, preferred_element_type=jnp.float32)
-    rows = jnp.sum(kept, axis=1, keepdims=True)
-    upper = jnp.dot(above, jnp.broadcast_to(rows, (n_home, 128)), preferred_element_type=jnp.float32)
-    ranks = (in_row + upper).astype(jnp.int32)
-    most = jnp.zeros((NZ, 1), jnp.float32)
+    f32, i32, bf = jnp.float32, jnp.int32, jnp.bfloat16
+
+    def iota(rows, cols, axis):
+        return lax.broadcasted_iota(i32, (rows, cols), axis)
+
+    def times(a, b):
+        return jnp.dot(a.astype(bf), b.astype(bf), preferred_element_type=f32)
+
+    t = tab[:, 0, :]
+    lane = iota(n_home, wide, 1)
+    home = iota(n_home, wide, 0)
+    kept = jnp.where((lane >= flags) & (lane < flags + BD), t, 0).astype(f32)
+    in_row = times(kept, (iota(wide, wide, 0) < iota(wide, wide, 1)).astype(f32))
+    count = jnp.broadcast_to(jnp.sum(kept, axis=1, keepdims=True), (n_home, wide))
+    upper = times(iota(n_home, n_home, 1) < iota(n_home, n_home, 0), count)
+    ranks = (in_row + upper).astype(i32)
+    first_rank = upper.astype(i32)
+
+    most = jnp.zeros((NZ, 1), f32)
     for c in range(NX):
         n = jnp.sum(jnp.where((ranks & (NX - 1)) == c, kept, 0.0), axis=1, keepdims=True)
         most = jnp.maximum(most, n[0:8] + n[8:16] + n[16:24] + n[24:32])
-    most = jnp.max(most)
-
-    for c in range(NZ):
-        cells[c] = 0
-
-    def wipe(i, carry):
-        for h in range(HD):
-            for u in range(8):
-                items[h * LFAST + i * 8 + u] = 0
-        return carry
-
-    lax.fori_loop(0, W_ALL // 8, wipe, 0)
+    most = jnp.max(most, axis=0, keepdims=True)
+    total = jnp.sum(count[:, 0:1], axis=0, keepdims=True)
+    row8 = iota(8, wide, 0)
+    info[...] = jnp.where(
+        row8 == 0, jnp.broadcast_to(total, (8, wide)), jnp.broadcast_to(most, (8, wide))
+    ).astype(i32)
+
+    row, line = home & (NZ - 1), home >> 3
+    blocks = []
+    mine_count = jnp.zeros((n_home, wide), f32)
+    for b in range(BD):
+        at = flags + b
+        k = jnp.broadcast_to(kept[:, at : at + 1], (n_home, wide)) > 0
+        r = jnp.broadcast_to(ranks[:, at : at + 1], (n_home, wide))
+        here = k & ((r >> 7) == window)
+        turn = jnp.where(((r - first_rank) >= 4) & (((r - 4) >> 7) == window), 1, 0)
+        mine = here & ((r & (NX - 1)) == x)
+        blocks.append((r, here, turn, mine))
+        mine_count = mine_count + jnp.where(mine, 1.0, 0.0)
+    same_row = (iota(n_home, n_home, 0) & (NZ - 1)) == (iota(n_home, n_home, 1) & (NZ - 1))
+    cell = times(same_row & (iota(n_home, n_home, 1) < iota(n_home, n_home, 0)), mine_count)
+    cell = cell.astype(i32) - part * TQ
+
+    send = jnp.zeros((n_home, wide), i32)
+    take = jnp.zeros((n_home, wide), i32)
+    hots, data = [], []
+    for b, (r, here, turn, mine) in enumerate(blocks):
+        send = send + jnp.where(here & (lane == (r & (NX - 1)) * 2 + turn), b, 0)
+        chosen = mine & (cell >= 0) & (cell < TQ)
+        take = take + jnp.where(chosen & (row == z) & (lane == cell), line * 2 + turn, 0)
+        hots.append(jnp.where(chosen & (((r >> 2) & 31) == lane), 1.0, 0.0))
+        moved = t if b == 0 else pltpu.roll(t, wide - R * b, 1)
+        moved = jnp.where(lane == 120, home * BD + b, moved)
+        moved = jnp.where(lane == 121, row * 8 + cell, moved)
+        data.append(jnp.where(lane == 122, 1, moved).astype(f32))
+        cell = cell + jnp.where(mine, 1, 0)
+    sendm[...] = send
+    take = jnp.sum(take.astype(f32), axis=0, keepdims=True).astype(i32)
+
+    hot = jnp.concatenate(hots, axis=0).astype(bf)
+    known = jnp.concatenate(data, axis=0).astype(bf)
+    of = lax.dot_general(hot, known, (((0,), (0,)), ((), ())), preferred_element_type=f32)
+    of = of[:32]
+
+    src, to = iota(wide, wide, 0), iota(wide, wide, 1)
+    kind = to & 7
+    wanted = jnp.where(kind < 3, 120, jnp.where(kind < 5, -1, (to >> 3) * (BD * R) + kind - 5))
+    tile = times(of, (src == wanted).astype(f32)).astype(i32)
+    spot = times(of, (src == 121).astype(f32)).astype(i32)
+    valid = times(of, (src == 122).astype(f32)) > 0.5
+    m = iota(32, wide, 1)
+    kind = m & 7
+    tile = tile + jnp.where(kind < 3, kind - 1, jnp.where(kind < 5, kind - 3, 0))
+    ok = valid & (m < 32) & (tile >= 0) & (tile < n_home * BD)
+    ok = ok & (((tile >> 3) & (NZ - 1)) == z)
+    hit = jnp.where(ok, 1.0, 0.0)
+    word = spot + ((((tile >> 6) & 3) * 8) + (tile & 7)) * 64
+    same_head = (src >> 3) == (to >> 3)
+    ahead = times(hit, (same_head & (src < to)).astype(f32))
+    whole = times(hit, same_head.astype(f32))
+    above = times(
+        times(iota(32, 32, 1) < iota(32, 32, 0), hit), same_head.astype(f32)
+    )
+    order = jnp.where(ok, (ahead + above).astype(i32), -1)
+    word = word + jnp.where(ahead < 0.5, 1 << 20, 0)
+    lastm[...] = jnp.where(whole > 0.5, (above + whole).astype(i32) - 1, W_ALL)
+
+    slots = iota(32, 2 * wide, 1)
     for h in range(HD):
-        for i in range(32):
-            last[h * 64 + i] = W_ALL
-    for c in range(9):
-        send_idx[c] = 0
-        comp[c] = 0
-
-    def one(home, carry):
-        rank, start = carry
-        zh, xh = home & (NZ - 1), home >> 3
-        start = jnp.where(home == s, rank, start)
-        used = xh * 2
-        cell = cells[zh]
-        here = zh == z
-        for b in range(BD):
-            k = tab[home, 0, flags + b]
-            mine = (k > 0) & ((rank & (NX - 1)) == x)
-            at = jnp.where(mine, rank >> 2, 64)
-            blk[at] = home * BD + b
-            slot[at] = zh * 8 + cell
-            comp[jnp.where(mine & here, cell, 8)] = used
-            add = jnp.where(mine, 1, 0)
-            used = used + add
-            cell = cell + add
-            rank = rank + k
-        cells[zh] = cell
-        return rank, start
-
-    total, start = lax.fori_loop(0, n_home, one, (jnp.int32(0), jnp.int32(0)))
-    fits = jnp.where(most <= 5.0, 2, jnp.where(most <= 6.0, 1, 0))
-    flag[0] = jnp.where(total <= 128, fits, 0)
-
-    filled = [jnp.int32(0)] * NX
-    rank = start
-    for j in range(BD):
-        k = tab[s, 0, flags + j]
-        col = rank & (NX - 1)
-        at = jnp.int32(8)
-        for c in range(NX):
-            hit = (k > 0) & (col == c)
-            at = jnp.where(hit, c * 2 + filled[c], at)
-            filled[c] = filled[c] + jnp.where(hit, 1, 0)
-        send_idx[at] = j
-        rank = rank + k
-
-    def query(a, cnt):
-        i = blk[a]
-        home, b = i >> 3, i & (BD - 1)
-        word = slot[a]
-        begin = [c + h * LFAST for h, c in enumerate(cnt)]
-        cnt = list(begin)
-
-        def add(h, w, one):
-            items[cnt[h]] = w + jnp.where(cnt[h] == begin[h], 1 << 20, 0)
-            cnt[h] = cnt[h] + one
-
-        for dt in (-1, 0, 1):
-            t = i + dt
-            near = t >> 3
-            ok = (t >= 0) & (t < n_home * BD) & ((near & (NZ - 1)) == z)
-            w = word + (((t >> 6) & 3) * 8 + (t & 7)) * 64
-            one = jnp.where(ok, 1, 0)
-            for h in range(HD):
-                add(h, w, one)
-        for h in range(HD):
-            for r in range(R):
-                t = tab[home, 0, h * BD * R + b * R + r]
-                w = word + ((t >> 6) * 8 + (t & 7)) * 64
-                add(h, w, jnp.where(((t >> 3) & (NZ - 1)) == z, 1, 0))
-
-        def with_shared(*cnt):
-            cnt = list(cnt)
-            for h in range(HD):
-                for g in range(G):
-                    items[cnt[h]] = word + g * 64 + jnp.where(cnt[h] == begin[h], 1 << 20, 0)
-                    cnt[h] = cnt[h] + 1
-            return tuple(cnt)
-
-        cnt = lax.cond(z == 0, with_shared, lambda *cnt: tuple(cnt), *cnt)
-        for h in range(HD):
-            last[h * 64 + a] = jnp.where(cnt[h] > begin[h], cnt[h] - 1 - h * LFAST, W_ALL)
-        return tuple(c - h * LFAST for h, c in enumerate(cnt))
-
-    n_mine = (total - x + NX - 1) >> 2
-    cnt = lax.fori_loop(0, n_mine, query, (jnp.int32(0),) * HD)
-    for h in range(HD):
-        items[h * LFAST + cnt[h]] = 0
-
-
-def fast_planned(tab):
-    i32 = lambda n: jax.ShapeDtypeStruct((n,), jnp.int32)
-    return pl.pallas_call(
-        fast_plan_kernel,
-        out_shape=[i32(16), i32(16), i32(HD * LFAST), i32(HD * 64), i32(8)],
-        in_specs=[SMEM_SPEC, VMEM_SPEC],
-        out_specs=[SMEM_SPEC] * 5,
-        scratch_shapes=[
-            pltpu.SMEM((72,), jnp.int32),
-            pltpu.SMEM((72,), jnp.int32),
-            pltpu.SMEM((NZ,), jnp.int32),
-        ],
-        compiler_params=params(None, 16),
-        name="fastplan",
-    )(tab, tab)
-
-
-NS = 4
+        found = jnp.zeros((32, 2 * wide), i32)
+        for k in range(8):
+            c = h * 8 + k
+            spots = jnp.broadcast_to(order[:, c : c + 1], (32, 2 * wide))
+            words = jnp.broadcast_to(word[:, c : c + 1], (32, 2 * wide))
+            found = found + jnp.where(spots == slots, words, 0)
+        found = (found[0:8] + found[8:16]) + (found[16:24] + found[24:32])
+        found = found[0:4] + found[4:8]
+        found = found[0:2] + found[2:4]
+        itemm[h : h + 1] = found[0:1] + found[1:2]
+    itemm[4:5] = jnp.concatenate([take, take], axis=1)
+
+
 EXP2 = score_scale * math.log2(math.e)
 Q_UP = [(k, h) for h in range(HD) for k in (1, 2, 3)] + [(4, 0), (4, 2)]
 Q_DOWN = [(k, h) for h in range(HD) for k in (1, 2, 3)] + [(4, 1), (4, 3)]
@@ -282,11 +214,13 @@
 M_DOWN = [(k, h) for h in range(HD) for k in (3, 2, 1)] + [(4, 0), (4, 2)]
 
 
-def main_kernel(tq, idx, comp, items, last, q_any, k_any, v_any, out, *rest):
+def main_kernel(turn, table_row, q_any, k_any, v_any, out, info, *rest):
     kvs, qrs, qzs, cos, cls = rest[0:4], rest[4:8], rest[8:12], rest[12:16], rest[16:20]
-    (qv, kbuf, vbuf, qs, res, rel, st_o, st_m, st_l, mo, ml, ro, rl, fin) = rest[20:34]
-    (load, sqx, rqx, skv, rkv, sfw, rfw, sq, rq, sm, rm, sx, rx) = rest[34:]
+    (qv, kbuf, vbuf, qs, sc, res, rel, st_o, st_m, st_l, mo, ml, ro, rl, fin) = rest[20:35]
+    (tab, sendm, lastm, itemm, sends, lasts, items) = rest[35:42]
+    (load, stab, rtab, sqx, rqx, skv, rkv, sfw, rfw, sq, rq, sm, rm, sx, rx) = rest[42:]
     s, x, z, hd = place()
+    n_seq = NX * NZ
 
     def at_x(d):
         return (lax.rem(x + d, NX) * NZ + z, hd)
@@ -307,16 +241,67 @@
     for copy in loads:
         copy.start()
     barrier = pltpu.get_barrier_semaphore()
-    for d in (1, 2, 3):
-        pl.semaphore_signal(barrier, inc=1, device_id=at_x(d), device_id_type=MESH)
-    for d in (1, -1):
-        pl.semaphore_signal(barrier, inc=1, device_id=at_z(d), device_id_type=MESH)
-
+    for d in range(1, n_seq):
+        pl.semaphore_signal(
+            barrier, inc=1, device_id=(lax.rem(s + d, n_seq), hd), device_id_type=MESH
+        )
+    tab[s] = table_row[...]
+    loads[1].wait()
+    loads[2].wait()
+
+    sent = []
+
+    def start(copy):
+        copy.start()
+        sent.append(copy)
+
+    gathers = []
+    for h in range(HD):
+        g = RowGather(kvs[h], (skv.at[h], rkv.at[h], sfw.at[h], rfw.at[h]), x, z, hd)
+        gathers.append(g)
+
+    def prepare(h):
+        def prep(b, carry):
+            rows = pl.ds(pl.multiple_of(b * B, B), B)
+            kvs[h][x, 0, b] = kbuf[rows, h * DH : (h + 1) * DH]
+            kvs[h][x, 1, b] = vbuf[rows, h * DH : (h + 1) * DH].T
+            return carry
+
+        lax.fori_loop(0, BD, prep, 0)
+
+
+    prepare(0)
+    pl.semaphore_wait(barrier, n_seq - 1)
+    gathers[0].own()
+    rows_out = []
+    for d in range(1, n_seq):
+        copy = pltpu.make_async_remote_copy(
+            src_ref=table_row,
+            dst_ref=tab.at[s],
+            send_sem=stab.at[d],
+            recv_sem=rtab.at[d],
+            device_id=(lax.rem(s + d, n_seq), hd),
+            device_id_type=MESH,
+        )
+        copy.start()
+        rows_out.append(copy)
+    prepare(1)
+    for copy in rows_out:
+        copy.wait()
+    plan(tab, turn[0], turn[1], s, x, z, sendm, lastm, itemm, info)
+    lists = [
+        pltpu.make_async_copy(src, dst, load.at[3 + i])
+        for i, (src, dst) in enumerate(((sendm, sends), (itemm, items), (lastm, lasts)))
+    ]
+    for copy in lists:
+        copy.start()
     loads[0].wait()
+    for copy in lists:
+        copy.wait()
 
     def fill(c, carry):
         col, u = c // 2, lax.rem(c, 2)
-        j = idx[c]
+        j = sends[s, c] & (BD - 1)
         for h in range(HD):
             qs[col, h, u] = qv[j, :, h * DH : (h + 1) * DH]
         return carry
@@ -325,13 +310,6 @@
     for h in range(HD):
         for u in range(2):
             qrs[h][x, u] = qs[x, h, u]
-    pl.semaphore_wait(barrier, 5)
-
-    sent = []
-
-    def start(copy):
-        copy.start()
-        sent.append(copy)
 
     def q_move(h, d, src):
         return pltpu.make_async_remote_copy(
@@ -343,28 +321,12 @@
             device_id_type=MESH,
         )
 
-    for h in range(HD):
+    def q_leave(h):
         for d in (1, 3, 2):
             start(q_move(h, d, xi(d)))
 
-    loads[1].wait()
-    loads[2].wait()
-    gathers = []
-    for h in range(HD):
-        g = RowGather(kvs[h], (skv.at[h], rkv.at[h], sfw.at[h], rfw.at[h]), x, z, hd)
-        gathers.append(g)
-
-    def prepare(h):
-        def prep(b, carry):
-            rows = pl.ds(pl.multiple_of(b * B, B), B)
-            kvs[h][x, 0, b] = kbuf[rows, h * DH : (h + 1) * DH]
-            kvs[h][x, 1, b] = vbuf[rows, h * DH : (h + 1) * DH].T
-            return carry
-
-        lax.fori_loop(0, BD, prep, 0)
-
-    prepare(0)
-    gathers[0].own()
+    q_leave(0)
+    q_leave(1)
 
     def q_copy(up, kk, h, row):
         n = (Q_UP if up else Q_DOWN).index((kk, h))
@@ -392,9 +354,9 @@
                 device_id=at_x(d),
                 device_id_type=MESH,
             ).wait_recv()
-        for c in range(tq):
-            w = comp[c]
-            qzs[h][z, c] = qrs[h][w >> 1, w & 1]
+        for c in range(TQ):
+            w = items[4, c]
+            qzs[h][z, c] = qrs[h][(w >> 1) & 3, w & 1]
 
     def q_begin(h):
         for up in (True, False):
@@ -411,30 +373,34 @@
     def chunk(h, part):
         kv, qz = kvs[h], qzs[h]
 
+        def words_of(n):
+            return [items[h, n * UN + u] for u in range(UN)]
+
+        def score(words):
+            for u, w in enumerate(words):
+                spot, tile = w & 63, (w >> 6) & 31
+                sc[u] = lax.dot_general(
+                    kv[tile >> 3, 0, tile & 7],
+                    qz[spot >> 3, jnp.minimum(spot & 7, TQ - 1)],
+                    (((1,), (1,)), ((), ())),
+                    preferred_element_type=jnp.float32,
+                )
+
         def batch(n, carry):
             m0, l0, o0 = st_m[...], st_l[...], st_o[...]
-            words = [items[h * LFAST + n * UN + u] for u in range(UN)]
-            scores = []
-            for w in words:
-                spot, tile = w & 63, (w >> 6) & 31
-                scores.append(
-                    lax.dot_general(
-                        kv[tile >> 3, 0, tile & 7],
-                        qz[spot >> 3, spot & 7],
-                        (((1,), (1,)), ((), ())),
-                        preferred_element_type=jnp.float32,
-                    )
-                )
+            words = words_of(n)
+            scores = [sc[u] for u in range(UN)]
             tops, weights = [], []
-            for sc in scores:
-                raw = jnp.max(sc, axis=0, keepdims=True)
+            for val in scores:
+                raw = jnp.max(val, axis=0, keepdims=True)
                 tops.append(raw)
-                weights.append(jnp.exp2((sc - raw) * EXP2).astype(jnp.bfloat16))
+                weights.append(jnp.exp2((val - raw) * EXP2).astype(jnp.bfloat16))
             sums = []
             for w, p in zip(words, weights):
                 tile = (w >> 6) & 31
                 rows = jnp.concatenate([kv[tile >> 3, 1, tile & 7], ones], axis=0)
                 sums.append(jnp.dot(rows, p, preferred_element_type=jnp.float32))
+            score(words_of(n + 1))
             for u, w in enumerate(words):
                 old = jnp.where((w >> 20) > 0, neg_big, m0)
                 top = jnp.maximum(old, tops[u])
@@ -449,11 +415,13 @@
             return carry
 
         ones = jnp.ones((16, B), jnp.bfloat16)
+        if part == 0:
+            score(words_of(0))
         lax.fori_loop(part * nb, (part + 1) * nb, batch, 0)
 
     def collect(h):
         for a in range(NZ * NS):
-            w = last[h * 64 + a]
+            w = jnp.clip(lasts[a, h * 8], 0, W_ALL)
             zp, i = (a >> 1) & 7, (a >> 4) * 2 + (a & 1)
             l = rel[w, 1:2]
             cos[h][zp, i] = (res[w] * (1.0 / l)).astype(jnp.bfloat16)
@@ -501,7 +469,6 @@
                 start(copy)
 
     def m_begin(h):
-        collect(h)
         m_step(4, h)
         for up in (True, False):
             table = M_UP if up else M_DOWN
@@ -567,72 +534,78 @@
     st_m[...] = jnp.full((1, B), neg_big, jnp.float32)
     st_l[...] = jnp.zeros((1, B), jnp.float32)
 
-    for h in (0, 1):
-        q_ready(h)
-        q_begin(h)
-    prepare(1)
-    q_ready(2)
-    q_ready(3)
-    q_step(1, 0)
-    q_step(1, 1)
     gathers[0].forward()
     gathers[1].own()
+    q_ready(0)
+    q_begin(0)
+    q_ready(1)
+    q_begin(1)
+    q_leave(2)
+    q_leave(3)
+    q_step(1, 0)
     prepare(2)
+    q_step(1, 1)
     prepare(3)
     q_step(2, 0)
+    gathers[1].forward()
+    gathers[2].own()
     q_step(2, 1)
     q_step(3, 0)
+    q_ready(2)
     q_step(3, 1)
     q_begin(2)
+    q_ready(3)
     q_begin(3)
     q_step(4, 0)
     gathers[0].finish()
     chunk(0, 0)
+    q_step(4, 1)
     q_step(1, 2)
     chunk(0, 1)
-    q_step(4, 1)
-    gathers[1].forward()
-    gathers[2].own()
+    gathers[2].forward()
+    gathers[3].own()
     q_step(1, 3)
     chunk(0, 2)
     q_step(2, 2)
     chunk(0, 3)
-    m_begin(0)
+    collect(0)
+    gathers[1].finish()
     q_step(2, 3)
-    gathers[1].finish()
     chunk(1, 0)
     q_step(3, 2)
+    gathers[3].forward()
     chunk(1, 1)
-    gathers[2].forward()
-    gathers[3].own()
     q_step(3, 3)
-    m_second(0)
+    m_begin(0)
     chunk(1, 2)
     q_step(4, 2)
+    chunk(1, 3)
+    collect(1)
+    m_begin(1)
     q_step(4, 3)
-    chunk(1, 3)
-    m_begin(1)
-    m_step(2, 0)
     gathers[2].finish()
+    m_second(0)
     chunk(2, 0)
     m_second(1)
     chunk(2, 1)
-    gathers[3].forward()
+    m_step(2, 0)
+    chunk(2, 2)
+    m_step(2, 1)
+    chunk(2, 3)
+    collect(2)
+    m_begin(2)
     m_step(1, 0)
-    m_step(2, 1)
-    chunk(2, 2)
-    chunk(2, 3)
-    m_begin(2)
-    m_step(1, 1)
-    m_end(0)
     gathers[3].finish()
     chunk(3, 0)
+    m_step(1, 1)
     m_second(2)
+    chunk(3, 1)
+    m_end(0)
+    chunk(3, 2)
+    m_step(2, 2)
     m_end(1)
-    chunk(3, 1)
-    m_step(2, 2)
-    chunk(3, 2)
     chunk(3, 3)
+    collect(3)
     m_begin(3)
     m_step(1, 2)
     m_second(3)
@@ -669,18 +642,22 @@
         copy.wait_send()
 
 
-def main_step(tq, idx, comp, items, last, q, k, v):
+def main_step(turn, row, q, k, v):
     dma = pltpu.SemaphoreType.DMA
     any_spec = pl.BlockSpec(memory_space=pl.ANY)
     bf, f32 = jnp.bfloat16, jnp.float32
-    out = pl.pallas_call(
-        functools.partial(main_kernel, tq),
-        out_shape=jax.ShapeDtypeStruct((2, NX, B, HD * DH), bf),
-        in_specs=[SMEM_SPEC] * 4 + [any_spec] * 3,
-        out_specs=VMEM_SPEC,
+    i32 = jnp.int32
+    out, info = pl.pallas_call(
+        main_kernel,
+        out_shape=[
+            jax.ShapeDtypeStruct((2, NX, B, HD * DH), bf),
+            jax.ShapeDtypeStruct((8, 128), i32),
+        ],
+        in_specs=[SMEM_SPEC, VMEM_SPEC] + [any_spec] * 3,
+        out_specs=[VMEM_SPEC] * 2,
         scratch_shapes=[pltpu.VMEM((NX, 2, BD, B, DH), bf)] * HD
         + [pltpu.VMEM((NX, 2, B, DH), bf)] * HD
-        + [pltpu.VMEM((NZ, tq, B, DH), bf)] * HD
+        + [pltpu.VMEM((NZ, TQ, B, DH), bf)] * HD
         + [pltpu.VMEM((NZ, NS, DH, B), bf)] * HD
         + [pltpu.VMEM((NZ, NS, 1, B), f32)] * HD
         + [
@@ -688,6 +665,7 @@
             pltpu.VMEM((BD * B, HD * DH), bf),
             pltpu.VMEM((BD * B, HD * DH), bf),
             pltpu.VMEM((NX, HD, 2, B, DH), bf),
+            pltpu.VMEM((UN, B, B), f32),
             pltpu.VMEM((W_ALL + 1, DH, B), f32),
             pltpu.VMEM((W_ALL + 1, 2, B), f32),
             pltpu.VMEM((DH, B), f32),
@@ -698,19 +676,26 @@
             pltpu.VMEM((2, 14, NS, DH, B), bf),
             pltpu.VMEM((2, 14, NS, 1, B), f32),
             pltpu.VMEM((HD, NS // 2, 2, B, DH), bf),
+            pltpu.VMEM((NX * NZ, 1, 128), i32),
+            pltpu.VMEM((NX * NZ, 128), i32),
+            pltpu.VMEM((32, 128), i32),
+            pltpu.VMEM((8, 256), i32),
+            pltpu.SMEM((NX * NZ, 128), i32),
+            pltpu.SMEM((32, 128), i32),
+            pltpu.SMEM((8, 256), i32),
         ]
         + [
-            dma((3,)),
+            dma((6,)), dma((NX * NZ,)), dma((NX * NZ,)),
             dma((4, HD)), dma((4, HD)),
             dma((HD, 2, 2)), dma((HD, 2, 2)), dma((HD, 2, 2)), dma((HD, 2, 2)),
             dma((2, 14)), dma((2, 14)),
             dma((2, 2, 14)), dma((2, 2, 14)),
             dma((HD, NS // 2)), dma((HD, 4)),
         ],
-        compiler_params=params(tq, 58),
-        name="main%d" % tq,
-    )(idx, comp, items, last, q, k, v)
-    return out.reshape(BD * B, HD * DH)
+        compiler_params=params(0, 58),
+        name="main",
+    )(turn, row, q, k, v)
+    return out.reshape(BD * B, HD * DH), info[0, 0], info[1, 0]
 
 
 def plan_kernel(tab, send_idx, items, counts, blk, slot):
@@ -1258,25 +1243,24 @@
 
 def body(queries, keys, values, random_holder, random_offset, keep):
     want = random_holder * BD + random_offset
-    row = jnp.concatenate([want.reshape(-1), keep, jnp.zeros((24,), jnp.int32)])
-    tab = gathered_table(row.reshape(1, 128))
+    row = jnp.concatenate([want.reshape(-1), keep, jnp.zeros((24,), jnp.int32)]).reshape(1, 128)
     q = queries.reshape(BD, B, HD * DH)
-    idx, comp, items, last, flag = fast_planned(tab)
-
-    def fast(tq):
-        def run(idx, comp, items, last, tab, q, keys, values):
-            return main_step(tq, idx, comp, items, last, q, keys, values)
-
-        return run
-
-    def wide(idx, comp, items, last, tab, q, keys, values):
-        send_idx, items, counts = planned(tab)
-        kv, qz = spread_all(send_idx, q, keys, values)
-        return joined(8, *parts_of(8, items, counts, kv, qz))
-
-    return lax.switch(
-        flag[0], (wide, fast(6), fast(5)), idx, comp, items, last, tab, q, keys, values
-    )
+    out, total, most = main_step(jnp.zeros((2,), jnp.int32), row, q, keys, values)
+    parts = (most + TQ - 1) // TQ
+    passes = (total + STEP - 1) // STEP * parts
+
+    def more(out):
+        def again(state):
+            n, out = state
+            turn = jnp.stack([n // parts, n % parts])
+            new = main_step(turn, row, q, keys, values)[0]
+            pairs = [(i, i + 2 * NZ) for i in range(2 * NZ)]
+            new = jnp.where(turn[0] > 0, lax.ppermute(new, "seq", pairs), new)
+            return n + 1, out + new
+
+        return lax.while_loop(lambda state: state[0] < passes, again, (jnp.int32(1), out))[1]
+
+    return lax.cond(passes > 1, more, lambda out: out, out)
 
 
 def solution(mesh):

time: 162 us -> 158 us (0.975)
  Pallas kernels: 159 us -> 152 us
  local copies, waits for them, and re-layouts: 1.18 us -> 3.62 us
    pallas_call x3 -> x1, Pallas kernels: 159 us -> 152 us  [main_step(): pl.pallas_call(main_kernel, out_shape=[jax.ShapeDtypeStruct((2, NX, B, HD...]
where the time goes in v4:
time: 158 us
  Pallas kernels  152 us (96%)
  local copies, waits for them, and re-layouts  3.62 us (2%)
    pallas_call x1, Pallas kernels, main_step(): pl.pallas_call(main_kernel, out_shape=[jax.ShapeDtypeStruct((2, NX, B, HD...  152 us

profile of v4, /device:TPU:24, one launch (start us, length us, event | category | flops | bytes accessed | tf_op | source)
XLA Modules:
  0.0 158.1 jit_solution(13894377120661299)
XLA Ops:
  0.0 0.7 multiply_add_fusion
  0.7 0.1 copy.10
  0.8 0.1 reshape.35
  0.9 0.0 copy-start.2
  0.9 0.6 copy-done.2
  1.6 0.1 add_bitcast_fusion.table_row
  1.7 0.5 broadcast_2_turn.2.turn
  2.2 0.0 copy-start
  2.2 0.0 copy-start.1
  2.2 152.1 %main.5 = (bf16[2,4,128,512]{3,2,1,0:T(8,128)(2,1)S(1)}, s32[8,128]{1,0:T(8,128)}) custom-call(s32[2]{0:T(128)} %broadcast_2_turn.2.turn, s32[1,128]{1,0:T(1,128)S(1)} %add_bitcast_fusion.table_row, bf16[8,128,512]{2,1,0:T(8,128)(2,1)} %bitcast.21, bf16[1024,512]{1,0:T(8,128)(2,1)} %k_any.1, bf16[1024,512]{1,0:T(8,128)(2,1)} %v_any.1), custom_call_target="tpu_custom_call" | custom-call | tf_op jit(solution)/shard_map/main/pallas_call | solution.py:650
  154.3 1.3 fusion
  156.9 0.0 copy-done
  156.9 0.0 copy-done.1
  156.9 0.2 conditional.1
  157.1 1.0 copy.20
  (1 shorter events, 0.0 us)
Async XLA Ops:
  0.9 0.7 copy-start.2
  2.2 154.7 %copy-start = (bf16[1024,512]{1,0:T(8,128)(2,1)S(1)}, bf16[1024,512]{1,0:T(8,128)(2,1)}, u32[]{:S(2)}) copy-start(bf16[1024,512]{1,0:T(8,128)(2,1)} %param.10) | copy-start | bytes 3145732
  2.2 154.7 %copy-start.1 = (bf16[1024,512]{1,0:T(8,128)(2,1)S(1)}, bf16[1024,512]{1,0:T(8,128)(2,1)}, u32[]{:S(2)}) copy-start(bf16[1024,512]{1,0:T(8,128)(2,1)} %k_any.1) | copy-start | bytes 3145732

commit v5 on v4

--- a/solution.py
+++ b/solution.py
@@ -17,6 +17,7 @@
 BD = 8
 TQ = 6
 NS = 4
+HALF = NS // 2
 UN = 8
 W_ANY = 128
 W_ALL = 192
@@ -68,8 +69,8 @@
         copy.start()
         self.sent.append(copy)
 
-    def own(self):
-        for order in (0, 1):
+    def own(self, orders=(0, 1)):
+        for order in orders:
             for side in (0, 1):
                 self.start(self.piece(0, side, order ^ side, self.x))
 
@@ -272,7 +273,7 @@
 
     prepare(0)
     pl.semaphore_wait(barrier, n_seq - 1)
-    gathers[0].own()
+    gathers[0].own((0,))
     rows_out = []
     for d in range(1, n_seq):
         copy = pltpu.make_async_remote_copy(
@@ -327,6 +328,7 @@
 
     q_leave(0)
     q_leave(1)
+    gathers[0].own((1,))
 
     def q_copy(up, kk, h, row):
         n = (Q_UP if up else Q_DOWN).index((kk, h))
@@ -427,69 +429,61 @@
             cos[h][zp, i] = (res[w] * (1.0 / l)).astype(jnp.bfloat16)
             cls[h][zp, i] = rel[w, 0:1] * score_scale + jnp.log(l)
 
-    def m_copies(up, kk, h, src_o, src_l):
+    def m_copies(up, kk, h, half, src_o, src_l):
         n = (M_UP if up else M_DOWN).index((kk, h))
         side = 0 if up else 1
+        part = slice(half * HALF, (half + 1) * HALF)
         return [
             pltpu.make_async_remote_copy(
-                src_ref=src,
-                dst_ref=dst.at[side, n],
-                send_sem=sm.at[i, side, n],
-                recv_sem=rm.at[i, side, n],
+                src_ref=src.at[part],
+                dst_ref=dst.at[side, n, part],
+                send_sem=sm.at[i, half, side, n],
+                recv_sem=rm.at[i, half, side, n],
                 device_id=at_z(1 if up else -1),
                 device_id_type=MESH,
             )
             for i, (src, dst) in enumerate(((src_o, ro), (src_l, rl)))
         ]
 
-    def m_arrived(up, kk, h):
+    def m_arrived(up, kk, h, half):
         n = (M_UP if up else M_DOWN).index((kk, h))
         side = 0 if up else 1
-        for copy in m_copies(up, kk, h, ro.at[side, n], rl.at[side, n]):
+        for copy in m_copies(up, kk, h, half, ro.at[side, n], rl.at[side, n]):
             copy.wait_recv()
         return side, n
 
+    def m_send(up, kk, h, half):
+        table = M_UP if up else M_DOWN
+        dest = zi(kk if up else -kk)
+        if (kk + 1, h) not in table:
+            for copy in m_copies(up, kk, h, half, cos[h].at[dest], cls[h].at[dest]):
+                start(copy)
+            return
+        side, prev = m_arrived(up, kk + 1, h, half)
+        n = table.index((kk, h))
+        for i in range(half * HALF, (half + 1) * HALF):
+            val, l = merged(cos[h][dest, i], cls[h][dest, i], ro[side, prev, i], rl[side, prev, i])
+            mo[side, n, i] = val.astype(jnp.bfloat16)
+            ml[side, n, i] = l
+        for copy in m_copies(up, kk, h, half, mo.at[side, n], ml.at[side, n]):
+            start(copy)
+
     def m_step(kk, h):
-        for up in (True, False):
-            table = M_UP if up else M_DOWN
-            if (kk, h) not in table:
-                continue
-            dest = zi(kk if up else -kk)
-            if (kk + 1, h) not in table:
-                for copy in m_copies(up, kk, h, cos[h].at[dest], cls[h].at[dest]):
-                    start(copy)
-                continue
-            side, prev = m_arrived(up, kk + 1, h)
-            n = table.index((kk, h))
-            for i in range(NS):
-                val, l = merged(cos[h][dest, i], cls[h][dest, i], ro[side, prev, i], rl[side, prev, i])
-                mo[side, n, i] = val.astype(jnp.bfloat16)
-                ml[side, n, i] = l
-            for copy in m_copies(up, kk, h, mo.at[side, n], ml.at[side, n]):
-                start(copy)
+        for half in (0, 1):
+            for up in (True, False):
+                m_send(up, kk, h, half)
 
     def m_begin(h):
-        m_step(4, h)
-        for up in (True, False):
-            table = M_UP if up else M_DOWN
-            if (4, h) not in table:
-                dest = zi(3 if up else -3)
-                for copy in m_copies(up, 3, h, cos[h].at[dest], cls[h].at[dest]):
-                    start(copy)
+        for half in (0, 1):
+            for up in (True, False):
+                longest = (4, h) in (M_UP if up else M_DOWN)
+                m_send(up, 4 if longest else 3, h, half)
 
     def m_second(h):
-        for up in (True, False):
-            table = M_UP if up else M_DOWN
-            if (4, h) in table:
-                dest = zi(3 if up else -3)
-                side, prev = m_arrived(up, 4, h)
-                n = table.index((3, h))
-                for i in range(NS):
-                    val, l = merged(cos[h][dest, i], cls[h][dest, i], ro[side, prev, i], rl[side, prev, i])
-                    mo[side, n, i] = val.astype(jnp.bfloat16)
-                    ml[side, n, i] = l
-                for copy in m_copies(up, 3, h, mo.at[side, n], ml.at[side, n]):
-                    start(copy)
+        for half in (0, 1):
+            for up in (True, False):
+                if (4, h) in (M_UP if up else M_DOWN):
+                    m_send(up, 3, h, half)
 
     def final(h, r, d):
         return pltpu.make_async_remote_copy(
@@ -504,24 +498,27 @@
     rows = NS // 2
 
     def m_end(h):
-        su, nu = m_arrived(True, 1, h)
-        sd, nd = m_arrived(False, 1, h)
         for i in range(NS):
+            if i % HALF == 0:
+                su, nu = m_arrived(True, 1, h, i // HALF)
+                sd, nd = m_arrived(False, 1, h, i // HALF)
             a, la = merged(ro[su, nu, i], rl[su, nu, i], ro[sd, nd, i], rl[sd, nd, i])
             val, _ = merged(cos[h][z, i], cls[h][z, i], a, la)
             fin[h, i // 2, i % 2] = val.T.astype(jnp.bfloat16)
-        for r in range(rows):
-
-            @pl.when(x == r)
-            def _(r=r):
-                for u in range(2):
-                    out[u, x, :, h * DH : (h + 1) * DH] = fin[h, r, u]
-
-            for d in (1, 2, 3):
-
-                @pl.when(lax.rem(x + d, NX) == r)
-                def _(r=r, d=d):
-                    final(h, r, d).start()
+            if i % 2 == 1:
+                leave(h, i // 2)
+
+    def leave(h, r):
+        @pl.when(x == r)
+        def _():
+            for u in range(2):
+                out[u, x, :, h * DH : (h + 1) * DH] = fin[h, r, u]
+
+        for d in (1, 2, 3):
+
+            @pl.when(lax.rem(x + d, NX) == r)
+            def _(d=d):
+                final(h, r, d).start()
 
     @pl.when(x >= rows)
     def _():
@@ -569,48 +566,48 @@
     q_step(2, 2)
     chunk(0, 3)
     collect(0)
+    m_begin(0)
     gathers[1].finish()
     q_step(2, 3)
     chunk(1, 0)
     q_step(3, 2)
+    m_second(0)
     gathers[3].forward()
     chunk(1, 1)
     q_step(3, 3)
-    m_begin(0)
+    m_step(2, 0)
     chunk(1, 2)
     q_step(4, 2)
     chunk(1, 3)
     collect(1)
     m_begin(1)
     q_step(4, 3)
+    m_step(1, 0)
     gathers[2].finish()
-    m_second(0)
     chunk(2, 0)
     m_second(1)
     chunk(2, 1)
-    m_step(2, 0)
+    m_end(0)
+    m_step(2, 1)
     chunk(2, 2)
-    m_step(2, 1)
     chunk(2, 3)
     collect(2)
     m_begin(2)
-    m_step(1, 0)
     gathers[3].finish()
     chunk(3, 0)
+    chunk(3, 1)
     m_step(1, 1)
     m_second(2)
-    chunk(3, 1)
-    m_end(0)
     chunk(3, 2)
-    m_step(2, 2)
-    m_end(1)
     chunk(3, 3)
     collect(3)
     m_begin(3)
+    m_step(2, 2)
+    m_end(1)
+    m_second(3)
     m_step(1, 2)
-    m_second(3)
+    m_step(2, 3)
     m_end(2)
-    m_step(2, 3)
     m_step(1, 3)
     m_end(3)
 
@@ -689,7 +686,7 @@
             dma((4, HD)), dma((4, HD)),
             dma((HD, 2, 2)), dma((HD, 2, 2)), dma((HD, 2, 2)), dma((HD, 2, 2)),
             dma((2, 14)), dma((2, 14)),
-            dma((2, 2, 14)), dma((2, 2, 14)),
+            dma((2, 2, 2, 14)), dma((2, 2, 2, 14)),
             dma((HD, NS // 2)), dma((HD, 4)),
         ],
         compiler_params=params(0, 58),

time: 158 us -> 156 us (0.987)
  Pallas kernels: 152 us -> 150 us
    pallas_call x1, Pallas kernels: 152 us -> 150 us  [main_step(): pl.pallas_call(main_kernel, out_shape=[jax.ShapeDtypeStruct((2, NX, B, HD...]
where the time goes in v5:
time: 156 us
  Pallas kernels  150 us (96%)
  local copies, waits for them, and re-layouts  3.62 us (2%)
    pallas_call x1, Pallas kernels, main_step(): pl.pallas_call(main_kernel, out_shape=[jax.ShapeDtypeStruct((2, NX, B, HD...  150 us

profile of v5, /device:TPU:24, one launch (start us, length us, event | category | flops | bytes accessed | tf_op | source)
XLA Modules:
  0.0 155.8 jit_solution(11683060502673257420)
XLA Ops:
  0.0 0.7 multiply_add_fusion
  0.7 0.1 copy.10
  0.8 0.1 reshape.35
  0.9 0.0 copy-start.2
  0.9 0.6 copy-done.2
  1.6 0.1 add_bitcast_fusion.table_row
  1.7 0.5 broadcast_2_turn.2.turn
  2.2 0.0 copy-start
  2.2 0.0 copy-start.1
  2.2 149.7 %main.5 = (bf16[2,4,128,512]{3,2,1,0:T(8,128)(2,1)S(1)}, s32[8,128]{1,0:T(8,128)}) custom-call(s32[2]{0:T(128)} %broadcast_2_turn.2.turn, s32[1,128]{1,0:T(1,128)S(1)} %add_bitcast_fusion.table_row, bf16[8,128,512]{2,1,0:T(8,128)(2,1)} %bitcast.21, bf16[1024,512]{1,0:T(8,128)(2,1)} %k_any.1, bf16[1024,512]{1,0:T(8,128)(2,1)} %v_any.1), custom_call_target="tpu_custom_call" | custom-call | tf_op jit(solution)/shard_map/main/pallas_call | solution.py:647
  151.9 1.3 fusion
  154.5 0.0 copy-done
  154.5 0.0 copy-done.1
  154.5 0.3 conditional.1
  154.8 1.0 copy.20
  (1 shorter events, 0.0 us)
Async XLA Ops:
  0.9 0.7 copy-start.2
  2.2 152.4 %copy-start = (bf16[1024,512]{1,0:T(8,128)(2,1)S(1)}, bf16[1024,512]{1,0:T(8,128)(2,1)}, u32[]{:S(2)}) copy-start(bf16[1024,512]{1,0:T(8,128)(2,1)} %param.10) | copy-start | bytes 3145732
  2.2 152.4 %copy-start.1 = (bf16[1024,512]{1,0:T(8,128)(2,1)S(1)}, bf16[1024,512]{1,0:T(8,128)(2,1)}, u32[]{:S(2)}) copy-start(bf16[1024,512]{1,0:T(8,128)(2,1)} %k_any.1) | copy-start | bytes 3145732
